TPU v7x, 128 devices: a whole 4x4x4 slice. The times are simulated.
128 devices in a mesh: section: 8 (over y, core), vocab: 16 (over x, z).
Axes of the slice: x: 4, y: 4, z: 4, core: 2. Of those that a mesh axis runs over, the one named last changes fastest.
Arguments:
- stream_in: bfloat16 [128, 5120], P(None, 'vocab'), may hold values from -20 to 20
- deltas: bfloat16 [16, 128, 5120], P('section', None, 'vocab'), may hold values from -6 to 6
- norm_gain: float32 [5120], P('vocab'), may hold values from 0.25 to 1.75
- unembed: bfloat16 [152064, 5120], P(('section', 'vocab')), may hold values from -0.559017 to 0.559017
- targets: int32 [128], replicated, may hold values from 0 to 152063
Outputs:
- lens_lse: float32 [16, 128], P('section')
- lens_entropy: float32 [16, 128], P('section')
- lens_logprob: float32 [16, 128], P('section')
All inputs are finite; a program needn't handle non-finite values.
Results may differ from a plain program's by a relative error of at most 0.0077.
Values may be sent and summed in bfloat16 or wider, within the bound.
A program may use at most 128 MiB of HBM per device.

v0:
```python
import functools

import jax
import jax.numpy as jnp
from jax import lax
from jax.sharding import Mesh
from jax.sharding import PartitionSpec as P

VOCAB = ("vocab_0", "vocab_1")
SECTION_VOCAB = ("section", "vocab_0", "vocab_1")


EPSILON = 1e-06


def from_everyone(value, axis):
    size = lax.axis_size(axis)
    return lax.all_to_all(
        jnp.broadcast_to(value[None], (size, *value.shape)), axis, 0, 0, tiled=True
    )


def joined_along(tiles, dim):
    tiles = jnp.moveaxis(tiles, 0, dim)
    lengths = tiles.shape
    return tiles.reshape(*lengths[:dim], lengths[dim] * lengths[dim + 1], *lengths[dim + 2 :])


def gathered_copies(value, axis, dim):
    tiles = from_everyone(value, axis)
    return joined_along(tiles, dim)


def over_axes(value, axes):
    return functools.reduce(lax.psum, axes, value)


def side_by_side(arrays, axis, split_dim, concat_dim, along):
    widths = [a.shape[along] for a in arrays]
    both = jnp.concatenate(arrays, axis=along)
    filled = lax.all_to_all(both, axis, split_axis=split_dim, concat_axis=concat_dim, tiled=True)
    return tuple(jnp.split(filled, [sum(widths[:k]) for k in range(1, len(widths))], axis=along))


def collected_together(value, axis):
    leaves = jax.tree.leaves(value)
    turns = sorted(range(len(leaves)), key=lambda k: -leaves[k].size)
    width = (1, *leaves[turns[0]].shape)[-1]
    lines = [
        jnp.pad(leaves[k].reshape(-1), (0, -leaves[k].size % width)).reshape(-1, width)
        for k in turns
    ]
    both, at, found = (from_everyone(jnp.concatenate(lines), axis), 0, {})
    for k, line in zip(turns, lines):
        share = both[:, at : at + len(line)].reshape(len(both), -1)
        found[k] = share[:, : leaves[k].size].reshape(-1, *leaves[k].shape)
        at += len(line)
    numbers = iter(range(len(leaves)))
    return jax.tree.map(lambda _: found[next(numbers)], value)


def folded_in_pairs(pieces, combine):
    while len(jax.tree.leaves(pieces)[0]) > 1:
        pieces = jax.vmap(combine)(
            *(jax.tree.map(lambda part: part[side::2], pieces) for side in (0, 1))
        )
    return jax.tree.map(lambda part: part[0], pieces)


def joined_all(value, axis, combine):
    pieces = collected_together(value, axis)
    return folded_in_pairs(pieces, combine)


def merge_pair(former, latter):
    peak_former, mass_former, moment_former, target_former = former
    peak_latter, mass_latter, moment_latter, target_latter = latter
    highest = jnp.maximum(peak_former, peak_latter)
    factor_former = jnp.exp(peak_former - highest)
    factor_latter = jnp.exp(peak_latter - highest)
    masses = mass_former * factor_former + mass_latter * factor_latter
    moments = moment_former * factor_former + moment_latter * factor_latter
    return (highest, masses, moments, target_former + target_latter)


def word_stats(logits, hit_mask):
    highest = jnp.max(logits, axis=1)
    weights = jnp.exp(logits - highest[:, None, :])
    masses = jnp.sum(weights, axis=1)
    moments = jnp.sum(weights * logits, axis=1)
    picked = jnp.sum(jnp.where(hit_mask[None], logits, 0.0), axis=1)
    return (highest, masses, moments, picked)


def shards(stream_in, deltas, norm_gain, unembed, targets):
    layers_own, tokens, width_dev = deltas.shape
    rows_dev = unembed.shape[0]
    section_index = lax.axis_index("section")
    own_first = section_index * layers_own
    first_word = (section_index * lax.axis_size(VOCAB) + lax.axis_index(VOCAB)) * rows_dev
    word_ids = first_word + lax.broadcasted_iota(jnp.int32, (rows_dev, tokens), 0)
    hit_mask = word_ids == targets[None, :]
    own_deltas = deltas.astype(jnp.float32)
    portion = gathered_copies(deltas, "section", 0)
    layer_ids = lax.broadcasted_iota(jnp.int32, (portion.shape[0], 1, 1), 0)
    kept_rows = jnp.where(layer_ids < own_first, portion.astype(jnp.float32), 0.0)
    lower_sum = jnp.sum(kept_rows, axis=0)
    residual = (
        stream_in.astype(jnp.float32)[None] + lower_sum[None] + jnp.cumsum(own_deltas, axis=0)
    )
    squares = over_axes(jnp.sum(residual * residual, axis=2), VOCAB)
    inverse_rms = lax.rsqrt(squares / (width_dev * lax.axis_size(VOCAB)) + EPSILON)
    normed = (residual * inverse_rms[:, :, None] * norm_gain[None, None, :]).astype(jnp.bfloat16)
    features = gathered_copies(normed, VOCAB, 2)
    logits = jnp.einsum(
        "wd,ltd->lwt",
        unembed,
        lax.all_gather(features, "section", axis=0, tiled=True),
        preferred_element_type=jnp.float32,
    )
    fresh_stats = word_stats(logits, hit_mask)
    statistics = tuple((after for after in fresh_stats))
    reshaped = tuple(
        (member.reshape(lax.axis_size("section"), layers_own, tokens) for member in statistics)
    )
    received = side_by_side(
        (reshaped[0], reshaped[1], reshaped[2], reshaped[3]), "section", 0, 0, 1
    )
    highest = jnp.max(received[0], axis=0)
    factor = jnp.exp(received[0] - highest[None])
    combined = (
        highest,
        jnp.sum(received[1] * factor, axis=0),
        jnp.sum(received[2] * factor, axis=0),
        jnp.sum(received[3], axis=0),
    )
    owned_stats = joined_all(combined, VOCAB, merge_pair)
    highest, masses, moments, picked = owned_stats
    lens_lse = highest + jnp.log(masses)
    entropy = lens_lse - moments / masses
    logprob = picked - lens_lse
    return (lens_lse, entropy, logprob)


def solution(mesh):
    torus = Mesh(
        mesh.devices.reshape(mesh.shape["section"], 4, 4), ("section", "vocab_0", "vocab_1")
    )
    placed = (P(None, VOCAB), P("section", None, VOCAB), P(VOCAB), P(SECTION_VOCAB, None), P())
    return jax.shard_map(
        shards,
        mesh=torus,
        in_specs=placed,
        out_specs=(P("section", None), P("section", None), P("section", None)),
        check_vma=False,
    )
```

profile of v0, /device:TPU:1, one launch (start us, length us, event | category | flops | bytes accessed | tf_op | source)
XLA Modules:
  0.0 256.8 jit_solution(4456421100557208478)
XLA Ops:
  7.2 2.2 broadcast_in_dim.31
  9.4 6.0 %all-to-all-start = ((bf16[8,2,128,320]{2,3,1,0:T(8,128)(2,1)}), bf16[8,2,128,320]{2,3,1,0:T(8,128)(2,1)S(1)}, u32[]{:S(2)}, u32[]{:S(2)}) async-start(bf16[8,2,128,320]{2,3,1,0:T(8,128)(2,1)} %broadcast_in_dim.31), calls=%async_computation | async-start | bytes 2621440 | tf_op jit(solution)/shard_map/all_to_all | solution.py:18
  15.4 0.0 all-gather.2.cloned.1.call-start
  15.4 17.8 %all-to-all-done = bf16[8,2,128,320]{2,3,1,0:T(8,128)(2,1)S(1)} async-done(((bf16[8,2,128,320]{2,3,1,0:T(8,128)(2,1)}), bf16[8,2,128,320]{2,3,1,0:T(8,128)(2,1)S(1)}, u32[]{:S(2)}, u32[]{:S(2)}) %all-to-all-start) | async-done | bytes 1310752 | tf_op jit(solution)/shard_map/all_to_all | solution.py:18
  33.1 0.3 select_reduce_fusion
  33.5 0.9 convert_add_fusion
  34.4 1.0 multiply_reduce_fusion
  35.4 8.5 %psum.14 = f32[2,128]{1,0:T(2,128)S(1)} all-reduce(f32[2,128]{1,0:T(2,128)S(1)} %get-tuple-element.22), channel_id=1, replica_groups=mesh['section'=8,'vocab_0'=4,'vocab_1'=4] {'vocab_0'}, use_global_device_ids=true, to_apply=%region_3.4 | all-reduce | flops 256 | bytes 2048 | tf_op jit(solution)/shard_map/psum | solution.py:35
  43.8 9.9 %psum.15 = f32[2,128]{1,0:T(2,128)S(1)} all-reduce(f32[2,128]{1,0:T(2,128)S(1)} %psum.14), channel_id=1, replica_groups=mesh['section'=8,'vocab_0'=4,'vocab_1'=4] {'vocab_1'}, use_global_device_ids=true, to_apply=%region_4.5 | all-reduce | flops 256 | bytes 2048 | tf_op jit(solution)/shard_map/psum | solution.py:35
  53.8 0.8 multiply_convert_fusion
  54.6 0.6 broadcast_in_dim.33
  55.2 0.0 copy-start.1
  55.2 31.7 %all_to_all.20 = bf16[16,2,128,320]{2,3,1,0:T(8,128)(2,1)S(1)} all-to-all(bf16[16,2,128,320]{2,3,1,0:T(8,128)(2,1)S(1)} %broadcast_in_dim.33), channel_id=1, replica_groups=mesh['section'=8,'vocab_0'=4,'vocab_1'=4] {'vocab_0','vocab_1'}, dimensions={0} | all-to-all | bytes 5242880 | tf_op jit(solution)/shard_map/all_to_all | solution.py:18
  86.8 0.2 copy.12
  87.0 2.7 %copy.13 = bf16[2,128,5120]{2,1,0:T(8,128)(2,1)} copy(bf16[2,128,5120]{1,2,0:T(8,128)(2,1)S(1)} %bitcast.37) | data formatting | bytes 5242880 | tf_op jit(solution)/shard_map/reshape | solution.py:26
  89.7 0.0 all-gather.2.cloned.1.call-update
  89.8 0.2 broadcast_compare_fusion
  90.0 104.0 %all-gather.2.cloned.1.call-done = bf16[16,128,5120]{2,1,0:T(8,128)(2,1)} async-done(((bf16[2,128,5120]{2,1,0:T(8,128)(2,1)}), bf16[16,128,5120]{2,1,0:T(8,128)(2,1)}) %all-gather.2.cloned.1.call-update) | async-done | bytes 20971536 | tf_op jit(solution)/shard_map/all_gather | solution.py:118
  194.0 30.1 %bitcast_reduce_fusion = (f32[16,128]{1,0:T(8,128)S(1)}, f32[16,128,1188]{1,2,0:T(8,128)S(1)}) fusion(bf16[16,128,5120]{2,1,0:T(8,128)(2,1)} %all-gather.2.cloned.1.call-done, bf16[1188,5120]{1,0:T(8,128)(2,1)} %param.8), kind=kOutput, calls=%fused_computation.5 | convolution fusion | flops 24916596736 | bytes 42876928 | tf_op jit(solution)/shard_map/wd,ltd->lwt/dot_general | solution.py:115
  224.2 2.7 %fusion.3 = (f32[16,128]{1,0:T(8,128)S(1)}, f32[16,128]{1,0:T(8,128)S(1)}, f32[16,128]{1,0:T(8,128)S(1)}) fusion(f32[16,128,1188]{1,2,0:T(8,128)S(1)} %get-tuple-element.25, f32[16,128]{1,0:T(8,128)S(1)} %get-tuple-element.24, pred[1188,128]{1,0:T(8,128)(4,1)S(1)} %broadcast_compare_fusion), kind=kLoop, calls=%fused_computation.7 | loop fusion | flops 14592000 | bytes 9916928 | tf_op jit(solution)/shard_map/reduce_sum | solution.py:89
  226.9 8.6 %all_to_all.21 = f32[8,8,128]{2,1,0:T(8,128)S(1)} all-to-all(f32[8,8,128]{2,1,0:T(8,128)S(1)} %pad_maximum_fusion), channel_id=1, replica_groups=mesh['section'=8,'vocab_0'=4,'vocab_1'=4] {'section'}, dimensions={0} | all-to-all | bytes 65536 | tf_op jit(solution)/shard_map/all_to_all | solution.py:41
  235.6 13.0 %all_to_all.22 = f32[16,8,128]{2,1,0:T(8,128)S(1)} all-to-all(f32[16,8,128]{2,1,0:T(8,128)S(1)} %broadcast_in_dim.56), channel_id=1, replica_groups=mesh['section'=8,'vocab_0'=4,'vocab_1'=4] {'vocab_0','vocab_1'}, dimensions={0} | all-to-all | bytes 131072 | tf_op jit(solution)/shard_map/all_to_all | solution.py:18
  248.8 0.6 fusion.10
  249.4 0.6 bitcast_subtract_fusion.1
  (20 shorter events, 0.3 us)
Async XLA Ops:
  9.4 23.7 %all-to-all-start = ((bf16[8,2,128,320]{2,3,1,0:T(8,128)(2,1)}), bf16[8,2,128,320]{2,3,1,0:T(8,128)(2,1)S(1)}, u32[]{:S(2)}, u32[]{:S(2)}) async-start(bf16[8,2,128,320]{2,3,1,0:T(8,128)(2,1)} %broadcast_in_dim.31), calls=%async_computation | async-start | bytes 2621440 | tf_op jit(solution)/shard_map/all_to_all | solution.py:18
  15.4 178.7 %all-gather.2.cloned.1.call-start = ((), (), s32[]{:S(2)}) async-start(), calls=%async_computation.4 | async-start | bytes 23592960 | tf_op jit(solution)/shard_map/all_gather | solution.py:118
  55.2 34.6 %copy-start.1 = (s32[128]{0:T(128)S(1)}, s32[128]{0:T(128)}, u32[]{:S(2)}) copy-start(s32[128]{0:T(128)} %param.9) | copy-start | bytes 1540
  249.4 0.6 copy-start
Sparse Core Ops, SparseCore 0:
  89.9 104.0 all-gather.1
where the time goes:
time: 258 us; the launch traced here: 257 us
  waiting for transfers between devices  122 us (47%)
  blocking collectives  71.7 us (28%)
  matrix products  30.1 us (12%)
  between operations  14.2 us (6%)
  other arithmetic  7.33 us (3%)
  starting transfers between devices  5.96 us (2%)
  local copies, waits for them, and re-layouts  5.75 us (2%)
    all_gather x1, waiting for transfers between devices, shards(): lax.all_gather(features, 'section', axis=0, tiled=True)  104 us
    all_to_all x2, blocking collectives, from_everyone(): lax.all_to_all(jnp.broadcast_to(value[None], (size, *value.shape)), axis,...  44.7 us
    dot_general x1, matrix products, shards(): jnp.einsum('wd,ltd->lwt', unembed, lax.all_gather(features, 'section', ax...  30.1 us
    psum x2, blocking collectives, over_axes(): return functools.reduce(lax.psum, axes, value)  18.4 us
    all_to_all x1, waiting for transfers between devices, from_everyone(): lax.all_to_all(jnp.broadcast_to(value[None], (size, *value.shape)), axis,...  17.8 us
    all_to_all x1, blocking collectives, side_by_side(): lax.all_to_all(both, axis, split_axis=split_dim, concat_axis=concat_dim,...  8.59 us
    all_to_all x1, starting transfers between devices, from_everyone(): lax.all_to_all(jnp.broadcast_to(value[None], (size, *value.shape)), axis,...  5.96 us
  transfers between devices with their start and end apart: 2, of which 2 were waited for; matrix products, arithmetic and copies ran while one was open for 0% of the time, Pallas kernels for 0%

commit v1 on v0

v1 whole, which is shorter than its diff:
```python
import functools

import jax
import jax.numpy as jnp
from jax import lax
from jax.experimental import pallas as pl
from jax.experimental.pallas import tpu as pltpu
from jax.sharding import Mesh
from jax.sharding import PartitionSpec as P

MESH = pl.DeviceIdType.MESH
F32 = jnp.float32
BF16 = jnp.bfloat16
EPSILON = 1e-06

VOCAB = ("vocab_0", "vocab_1")
SECTION_VOCAB = ("section", "vocab_0", "vocab_1")

LINKS = ((0, 1), (0, -1), (1, 1), (1, -1), (2, 1), (2, -1))
TREE = (
    (-1, 0, 0, 1), (0, -1, 0, 3), (0, 0, -1, 5), (0, 0, 1, 4), (0, 1, 0, 2), (1, 0, 0, 0),
    (-1, -1, 0, 1), (0, -1, -1, 3), (0, 0, 2, 4), (0, 1, -1, 5), (2, 0, 0, 0), (-1, 0, -1, 5),
    (0, 1, 1, 4), (0, 2, 0, 3), (1, 0, 1, 0), (-1, 0, 1, 1), (0, -1, 1, 4), (1, -1, 0, 3),
    (1, 1, 0, 0), (-1, 1, 0, 1), (0, 1, 2, 2), (0, -1, 2, 5), (1, 1, -1, 0), (2, -1, 0, 1),
    (-1, 1, -1, 2), (-1, 2, 0, 3), (0, 2, 1, 4), (1, 0, 2, 0), (2, 0, -1, 5), (1, 1, 1, 2),
    (-1, 1, 1, 1), (0, 2, -1, 5), (1, -1, 1, 4), (2, 0, 1, 0), (1, 2, 0, 2), (-1, -1, -1, 1),
    (-1, -1, 1, 4), (1, -1, -1, 5), (1, 0, -1, 0), (1, 2, -1, 2), (-1, -1, 2, 1), (0, 2, 2, 3),
    (1, 1, 2, 5), (2, -1, 1, 4), (2, 1, -1, 0), (-1, 2, -1, 2), (-1, 2, 1, 1), (1, 2, 1, 0),
    (2, -1, -1, 3), (2, 1, 0, 2), (-1, 0, 2, 1), (1, -1, 2, 3), (2, 0, 2, 4), (2, 1, 1, 2),
    (-1, 1, 2, 4), (2, 2, 0, 3), (1, 2, 2, 2), (2, 1, 2, 5), (2, 2, 1, 3), (-1, 2, 2, 3),
    (2, -1, 2, 5), (2, 2, -1, 1), (2, 2, 2, 4),
)
PLAN = (
    (
        (
            (1, 0, 0), (1, 0, 1), (1, 1, 0), (1, 1, 1), (1, 2, 0), (1, 2, 1), (1, 3, 0), (1, 3, 1), (1, 4, 0),
            (1, 4, 1), (1, 5, 0), (1, 5, 1), (1, 0, 2), (1, 1, 2), (1, 2, 2), (1, 3, 2), (1, 4, 2), (1, 5, 2),
            (1, 0, 3), (1, 1, 3), (1, 2, 3), (1, 3, 3), (1, 4, 3), (1, 5, 3), (0, 0, 0), (0, 1, 0), (0, 2, 0),
            (0, 3, 0), (0, 4, 0), (0, 5, 0), (1, 6, 0), (1, 7, 0), (1, 8, 0), (1, 9, 0), (1, 10, 0), (1, 11, 0),
            (1, 12, 0), (1, 13, 0), (1, 14, 0), (1, 15, 0), (1, 16, 0), (1, 17, 0), (1, 18, 0), (0, 0, 1), (0, 1, 1),
            (0, 2, 1), (0, 3, 1), (0, 4, 1), (0, 5, 1), (1, 6, 1), (1, 9, 1), (1, 7, 1), (1, 8, 1), (1, 10, 1),
            (1, 11, 1), (1, 19, 0), (0, 0, 2), (0, 1, 2), (0, 2, 2), (0, 3, 2), (0, 4, 2), (0, 5, 2), (1, 12, 1),
            (1, 13, 1), (0, 0, 3), (0, 1, 3), (0, 2, 3), (0, 3, 3), (0, 4, 3), (0, 5, 3), (0, 6, 0), (0, 7, 0),
            (0, 8, 0), (0, 9, 0), (0, 10, 0), (1, 20, 0), (1, 21, 0), (1, 22, 0), (1, 23, 0), (1, 25, 0), (1, 27, 0),
            (1, 28, 0), (1, 17, 1), (0, 6, 1), (0, 11, 0), (0, 12, 0), (0, 13, 0), (0, 14, 0), (1, 23, 1), (1, 24, 0),
            (1, 26, 0), (1, 29, 0), (1, 30, 0), (1, 31, 0), (1, 33, 0), (1, 7, 2), (1, 35, 0), (1, 36, 0), (1, 38, 0),
            (0, 9, 1), (0, 15, 0), (0, 16, 0), (0, 17, 0), (0, 18, 0), (1, 32, 0), (1, 34, 0), (1, 37, 0), (0, 7, 1),
            (0, 8, 1), (0, 10, 1), (0, 11, 1), (0, 19, 0), (0, 20, 0), (1, 21, 1), (0, 12, 1), (0, 13, 1), (0, 21, 0),
            (0, 22, 0), (0, 23, 0), (1, 39, 0), (1, 40, 0), (1, 41, 0), (1, 42, 0), (1, 43, 0), (1, 44, 0), (1, 49, 0),
            (0, 24, 0), (1, 45, 0), (1, 14, 1), (1, 28, 1), (1, 50, 0), (0, 23, 1), (0, 25, 0), (0, 26, 0), (0, 27, 0),
            (0, 28, 0), (1, 43, 1), (1, 46, 0), (1, 47, 0), (1, 48, 0), (1, 51, 0), (0, 29, 0), (1, 6, 2), (1, 9, 2),
            (1, 22, 1), (1, 55, 0), (0, 17, 1), (0, 30, 0), (0, 31, 0), (0, 32, 0), (0, 33, 0), (1, 52, 0), (1, 53, 0),
            (1, 54, 0), (0, 34, 0), (1, 18, 1), (1, 26, 1), (1, 30, 1), (0, 7, 2), (0, 35, 0), (0, 36, 0), (0, 37, 0),
            (0, 38, 0), (1, 24, 1), (0, 39, 0), (1, 16, 1), (1, 27, 1), (0, 40, 0), (0, 41, 0), (0, 42, 0), (0, 43, 0),
            (0, 44, 0),
        ),
        (
            (1, 56, 0), (1, 57, 0), (1, 58, 0), (1, 59, 0), (1, 20, 1), (0, 45, 0), (1, 61, 0), (1, 11, 2), (1, 32, 1),
            (0, 21, 1), (0, 43, 1), (0, 46, 0), (0, 47, 0), (0, 48, 0), (1, 40, 1), (1, 60, 0),
        ),
        (
            (0, 49, 0), (1, 8, 2), (1, 58, 1), (0, 14, 1), (0, 28, 1), (0, 50, 0), (0, 51, 0), (0, 52, 0), (1, 33, 1),
            (1, 48, 1), (1, 29, 1),
        ),
    ),
    (
        (
            (0, 53, 0), (1, 10, 2), (1, 31, 1), (1, 41, 1), (0, 6, 2), (0, 9, 2), (0, 22, 1), (0, 54, 0), (0, 55, 0),
            (1, 23, 2), (1, 39, 1), (1, 42, 1), (1, 44, 1), (0, 56, 0),
        ),
        (
            (1, 12, 2), (1, 35, 1), (1, 37, 1), (0, 18, 1), (0, 26, 1), (0, 30, 1), (0, 57, 0), (0, 58, 0), (1, 46, 1),
            (1, 47, 1), (1, 62, 0), (1, 34, 1), (0, 24, 1), (1, 45, 1), (1, 15, 1), (1, 38, 1), (1, 55, 1),
        ),
        (
            (0, 16, 1), (0, 27, 1), (0, 59, 0), (0, 60, 0), (0, 61, 0), (1, 51, 1), (0, 20, 1), (1, 13, 2), (1, 14, 2),
            (1, 19, 1), (0, 11, 2), (0, 32, 1), (0, 33, 1), (0, 40, 1), (0, 48, 1),
        ),
    ),
    (
        (),
        (
            (1, 52, 1), (1, 60, 1), (1, 49, 1), (0, 39, 1), (1, 21, 2), (1, 22, 2), (1, 25, 1), (1, 50, 1), (0, 8, 2),
            (0, 23, 2), (0, 42, 1), (0, 44, 1), (0, 58, 1), (1, 43, 2), (1, 56, 1), (1, 57, 1), (1, 62, 1), (1, 53, 1),
        ),
        (
            (0, 29, 1), (1, 18, 2), (1, 54, 1), (1, 59, 1), (0, 10, 2), (0, 31, 1), (0, 41, 1), (0, 46, 1), (0, 62, 0),
            (1, 28, 2), (1, 24, 2),
        ),
    ),
    (
        (),
        (
            (0, 45, 1), (1, 61, 1), (1, 6, 3), (1, 9, 3), (1, 17, 2), (1, 27, 2), (1, 36, 1), (0, 12, 2), (0, 35, 1),
            (0, 37, 1), (0, 47, 1), (0, 51, 1), (1, 20, 2), (0, 34, 1), (1, 7, 3), (1, 11, 3), (1, 30, 2),
        ),
        (
            (0, 15, 1), (0, 38, 1), (0, 52, 1), (0, 55, 1), (0, 60, 1), (0, 56, 1), (1, 16, 2),
        ),
    ),
    (
        (
            (0, 13, 2), (0, 14, 2), (0, 19, 1), (0, 57, 1), (0, 62, 1), (1, 26, 2), (1, 33, 2), (1, 29, 2), (0, 49, 1),
            (1, 8, 3), (1, 10, 3), (1, 31, 2), (1, 35, 2),
        ),
        (
            (0, 21, 2), (0, 22, 2), (0, 25, 1), (0, 43, 2), (0, 50, 1), (1, 39, 2), (1, 40, 2), (1, 42, 2), (1, 44, 2),
            (1, 58, 2), (0, 53, 1), (1, 38, 2), (1, 41, 2), (0, 18, 2), (0, 28, 2), (0, 54, 1), (0, 59, 1), (0, 61, 1),
            (1, 48, 2),
        ),
        (
            (1, 34, 2), (0, 24, 2), (1, 45, 2), (0, 6, 3), (0, 9, 3), (0, 17, 2), (0, 27, 2), (0, 36, 1), (1, 23, 3),
            (1, 32, 2), (1, 37, 2), (1, 51, 2),
        ),
    ),
    (
        (),
        (
            (0, 20, 2), (1, 14, 3), (1, 15, 2), (1, 55, 2), (0, 7, 3), (0, 11, 3), (0, 26, 2), (0, 30, 2), (0, 33, 2),
            (1, 21, 3), (1, 46, 2), (1, 47, 2), (1, 52, 2), (1, 49, 2), (0, 39, 2),
        ),
        (
            (1, 12, 3), (1, 13, 3), (1, 19, 2), (1, 22, 3), (0, 16, 2), (0, 40, 2), (0, 42, 2), (0, 44, 2), (0, 58, 2),
            (1, 56, 2), (1, 57, 2), (1, 62, 2), (1, 53, 2), (0, 29, 2),
        ),
    ),
    (
        (),
        (
            (1, 18, 3), (1, 25, 2), (0, 8, 3), (0, 10, 3), (0, 31, 2), (0, 35, 2), (0, 48, 2), (1, 28, 3), (1, 60, 2),
            (1, 24, 3), (0, 45, 2), (1, 61, 2), (1, 27, 3), (1, 50, 2), (1, 54, 2), (1, 59, 2), (0, 23, 3), (0, 32, 2),
            (0, 37, 2), (0, 38, 2), (0, 41, 2), (1, 43, 3),
        ),
        (
            (1, 20, 3), (0, 34, 2), (1, 17, 3), (1, 36, 2), (0, 21, 3), (0, 46, 2), (0, 47, 2), (0, 51, 2), (0, 52, 2),
            (1, 40, 3),
        ),
    ),
    (
        (),
        (
            (0, 56, 2), (1, 41, 3), (0, 14, 3), (0, 15, 2), (0, 55, 2), (0, 57, 2), (0, 62, 2), (1, 33, 3), (1, 29, 3),
        ),
        (
            (0, 49, 2), (1, 16, 3), (1, 35, 3), (1, 38, 3), (0, 12, 3), (0, 13, 3), (0, 19, 2), (0, 22, 3), (0, 60, 2),
            (1, 26, 3), (1, 30, 3), (1, 31, 3), (1, 39, 3), (1, 42, 3), (1, 44, 3),
        ),
    ),
    (
        (
            (0, 53, 2), (1, 15, 3), (1, 36, 3), (0, 18, 3), (0, 25, 2), (0, 28, 3), (0, 43, 3), (0, 61, 2), (1, 48, 3),
            (1, 58, 3), (1, 34, 3),
        ),
        (
            (0, 24, 3), (1, 45, 3), (1, 19, 3), (0, 27, 3), (0, 50, 2), (0, 54, 2), (0, 59, 2), (1, 51, 3), (0, 20, 3),
            (1, 55, 3),
        ),
        (
            (0, 17, 3), (0, 33, 3), (0, 36, 2), (0, 40, 3), (1, 32, 3), (1, 37, 3), (1, 52, 3), (1, 49, 3), (0, 39, 3),
            (0, 42, 3), (1, 56, 3), (1, 25, 3), (1, 50, 3),
        ),
    ),
    (
        (),
        (
            (0, 26, 3), (0, 30, 3), (0, 41, 3), (0, 44, 3), (1, 46, 3), (1, 47, 3), (1, 54, 3), (1, 57, 3), (1, 53, 3),
            (0, 29, 3), (0, 31, 3), (1, 59, 3), (0, 16, 3), (0, 35, 3), (0, 38, 3), (0, 48, 3), (1, 60, 3),
        ),
        (
            (0, 45, 3), (1, 61, 3), (0, 15, 3), (0, 36, 3), (0, 58, 3), (1, 62, 3),
        ),
    ),
    (
        (),
        (
            (0, 34, 3), (0, 37, 3), (0, 19, 3), (0, 32, 3), (0, 51, 3), (0, 47, 3), (0, 56, 3), (0, 57, 3),
        ),
        (
            (0, 46, 3), (0, 52, 3), (0, 55, 3), (0, 49, 3), (0, 60, 3),
        ),
    ),
    (
        (),
        (
            (0, 25, 3), (0, 50, 3), (0, 54, 3), (0, 53, 3), (0, 59, 3), (0, 61, 3), (0, 62, 3),
        ),
        (),
    ),
    (
        (),
        (),
        (),
    ),
    (
        (),
        (),
        (),
    ),
    (
        (),
        (),
        (),
    ),
    (
        (),
        (),
        (),
    ),
)
PLANES = (0, 1, -1, 2)

GROUPS = 4
GTOK = 16
FILL = -1e30


def pick(index, values):
    out = values[-1]
    for k in range(len(values) - 2, -1, -1):
        out = jnp.where(index == k, values[k], out)
    return out


def dispatch(index, branches, low=0, high=None):
    high = len(branches) if high is None else high
    if not any(branches[low:high]):
        return
    if high - low == 1:
        branches[low]()
        return
    mid = (low + high) // 2

    @pl.when(index < mid)
    def _():
        dispatch(index, branches, low, mid)

    @pl.when(index >= mid)
    def _():
        dispatch(index, branches, mid, high)


def kernel(
    stream_hbm, deltas_hbm, gain_hbm, unembed_hbm, targets_hbm, out_ref,
    stream_v, deltas_v, targets_v, gains, outbox, gat, words, rows, acc, squares,
    stats, from_x, stats_x, from_y, stats_y, from_z,
    load_sem, own_sem, words_send, words_recv, gain_send, gain_recv,
    part_send, part_recv, send_sem, recv_sem,
    x_send, x_recv, y_send, y_recv, z_send, z_recv,
):
    section = lax.axis_index("section")
    x = lax.axis_index("vocab_0")
    z = lax.axis_index("vocab_1")
    y = section // 2
    core = section % 2
    sign = 1 - 2 * core
    nwords = unembed_hbm.shape[0]
    plane_width = unembed_hbm.shape[1] // 4
    home = (x, y, z)

    def device(xx, yy, zz, cc):
        return (yy * 2 + cc, xx, zz)

    def moved(axis, step):
        at = list(home)
        at[axis] = lax.rem(at[axis] + step + 4, 4)
        return tuple(at)

    neighbours = [device(*moved(axis, way * sign), core) for axis, way in LINKS]
    partner = device(x, y, z, 1 - core)
    source = [{d: lax.rem(home[axis] - sign * d + 4, 4) for d in (-1, 0, 1, 2)} for axis in range(3)]

    loads = [
        pltpu.make_async_copy(stream_hbm, stream_v, load_sem.at[0]),
        pltpu.make_async_copy(deltas_hbm, deltas_v, load_sem.at[1]),
        pltpu.make_async_copy(targets_hbm, targets_v, load_sem.at[2]),
        pltpu.make_async_copy(gain_hbm, gains.at[x * 4 + z], load_sem.at[3]),
    ]
    for copy in loads:
        copy.start()

    barrier = pltpu.get_barrier_semaphore()
    for axis in range(3):
        for step in (1, 2, 3):
            at = moved(axis, step)
            pl.semaphore_signal(barrier, inc=1, device_id=device(*at, core), device_id_type=MESH)
            if axis == 2:
                pl.semaphore_signal(barrier, inc=1, device_id=device(*at, 1 - core), device_id_type=MESH)
    pl.semaphore_signal(barrier, inc=1, device_id=partner, device_id_type=MESH)

    def columns(plane):
        return pl.ds(pl.multiple_of(plane * plane_width, 128), plane_width)

    own_words = []
    for p, dx in enumerate(PLANES):
        plane = source[0][dx]
        own_words.append(
            pltpu.make_async_copy(
                unembed_hbm.at[:, columns(plane)], words.at[0, plane, pl.ds(0, nwords)], own_sem.at[p]
            )
        )
        own_words[-1].start()

    for copy in loads:
        copy.wait()

    lane = lax.broadcasted_iota(jnp.int32, (GTOK, 128), 1)
    low = lane < 64
    odd = lax.rem(z, 2) == 1
    first = jnp.where(section == 0, 1.0, 0.0).astype(F32)
    my_slot = ((x * 4 + y) * 4 + z) * GROUPS
    for half in range(2):
        for g in range(GROUPS):
            t0 = half * 64 + g * GTOK
            tiles = []
            for k in range(3):
                cols = slice(128 * k, min(128 * k + 128, 320))
                base = stream_v[t0 : t0 + GTOK, cols].astype(F32)
                former = deltas_v[0, t0 : t0 + GTOK, cols].astype(F32) + base * first
                kept = former.astype(BF16).astype(F32)
                latter = deltas_v[1, t0 : t0 + GTOK, cols].astype(F32) + (former - kept)
                pair = [kept, latter]
                if k == 2:
                    pair = [jnp.concatenate([v, jnp.zeros_like(v)], axis=1) for v in pair]
                tiles.append(pair)
            packed = []
            heads = []
            for l in range(2):
                a0, a1, a2 = (tiles[k][l] for k in range(3))
                r0, r1, r2 = (pltpu.roll(v, 64, 1) for v in (a0, a1, a2))
                packed.append(jnp.where(odd, jnp.where(low, r0, r1), a0))
                packed.append(jnp.where(odd, jnp.where(low, r1, r2), a1))
                heads.append(jnp.where(odd, a0, a2))
            lead = jnp.where(odd, heads[1], heads[0])
            trail = jnp.where(odd, heads[0], heads[1])
            packed.append(jnp.where(low, lead, pltpu.roll(trail, 64, 1)))

            @pl.when(core == half)
            def _():
                for k, value in enumerate(packed):
                    gat[my_slot + g, core, k] = value.astype(BF16)

            @pl.when(core != half)
            def _():
                for k, value in enumerate(packed):
                    outbox[g, k] = value.astype(BF16)

    acc[:, 1184:1200, :] = jnp.full((2, 16, 256), FILL, F32)

    pl.semaphore_wait(barrier, 13)

    part = pltpu.make_async_remote_copy(
        src_ref=outbox,
        dst_ref=gat.at[pl.ds(my_slot, GROUPS), core],
        send_sem=part_send,
        recv_sem=part_recv,
        device_id=partner,
        device_id_type=MESH,
    )
    part.start()

    def gain_copy(n, link):
        at = (source[0][n[0]] * 4 + source[2][n[2]])
        place = (TREE_INDEX[child(n, link)] if link is not None else TREE_INDEX[n])
        return pltpu.make_async_remote_copy(
            src_ref=gains.at[at],
            dst_ref=gains.at[at],
            send_sem=gain_send.at[GAIN_INDEX[place]],
            recv_sem=gain_recv.at[GAIN_INDEX[place]],
            device_id=neighbours[link or 0],
            device_id_type=MESH,
        )

    def block_copy(n, row, link, g):
        slot = source[0][n[0]] * 64 + source[1][n[1]] * 16 + source[2][n[2]] * 4 + g
        return pltpu.make_async_remote_copy(
            src_ref=gat.at[slot],
            dst_ref=gat.at[slot],
            send_sem=send_sem.at[g],
            recv_sem=recv_sem.at[row * GROUPS + g],
            device_id=neighbours[link],
            device_id_type=MESH,
        )

    def send_gain(n):
        for row, (dx, dy, dz, link) in enumerate(TREE):
            if dy == 0 and parent((dx, dy, dz), link) == n:
                gain_copy(n, link).start()

    def run(actions):
        for kind, row, g in actions:
            dx, dy, dz, link = TREE[row]
            n = (dx, dy, dz)
            if kind == 0:
                block_copy(n, row, link, g).wait_recv()
                if g == 0 and dy == 0:
                    gain_copy(n, None).wait_recv()
                    send_gain(n)
            else:
                block_copy(parent(n, link), row, link, g).start()

    send_gain((0, 0, 0))

    their_words = []
    for p, dx in enumerate(PLANES):
        plane = lax.rem(x + sign * dx + 4, 4)
        their_words.append(
            pltpu.make_async_remote_copy(
                src_ref=unembed_hbm.at[:, columns(plane)],
                dst_ref=words.at[1, plane, pl.ds(0, nwords)],
                send_sem=words_send.at[p],
                recv_sem=words_recv.at[p],
                device_id=partner,
                device_id_type=MESH,
            )
        )

    part.wait_recv()
    their_words[0].start()
    their_words[1].start()
    their_words[2].start()
    their_words[3].start()

    def body(s, carry):
        g = s // 4
        p = lax.rem(s, 4)
        plane = pick(p, [source[0][dx] for dx in PLANES])
        dispatch(s, [functools.partial(run, step[0]) if step[0] else None for step in PLAN])

        running = [jnp.zeros((GTOK, 128), F32) for _ in range(10)]
        gain_rows = []
        for zp in range(2):
            both = gains[plane * 4 + 2 * zp] + gains[plane * 4 + 2 * zp + 1]
            gain_rows.extend(jnp.broadcast_to(both[k : k + 1, :], (GTOK, 128)) for k in range(5))
        for yy in range(4):
            for cc in range(2):
                blocks = []
                for zz in range(4):
                    slot = plane * 64 + yy * 16 + zz * 4 + g
                    blocks.append(slot)
                for l in range(2):
                    layer = 4 * yy + 2 * cc + l
                    total = jnp.zeros((GTOK, 128), F32)
                    for zp in range(2):
                        even, other = blocks[2 * zp], blocks[2 * zp + 1]
                        pe = gat[even, cc, 4].astype(F32)
                        po = gat[other, cc, 4].astype(F32)
                        if l == 0:
                            middle = jnp.where(low, pe, po)
                        else:
                            middle = pltpu.roll(jnp.where(low, po, pe), 64, 1)
                        values = [
                            gat[even, cc, 2 * l].astype(F32),
                            gat[even, cc, 2 * l + 1].astype(F32),
                            middle,
                            gat[other, cc, 2 * l].astype(F32),
                            gat[other, cc, 2 * l + 1].astype(F32),
                        ]
                        for k in range(5):
                            at = 5 * zp + k
                            running[at] = running[at] + values[k]
                            total = total + running[at] * running[at]
                            rows[layer * GTOK : (layer + 1) * GTOK, at * 128 : (at + 1) * 128] = (
                                running[at] * gain_rows[at]
                            ).astype(BF16)
                    former = squares[layer * GTOK : (layer + 1) * GTOK, :]
                    squares[layer * GTOK : (layer + 1) * GTOK, :] = jnp.where(p == 0, 0.0, former) + total

        @pl.when(s < 4)
        def _():
            pltpu.make_async_copy(
                unembed_hbm.at[:, columns(plane)], words.at[0, plane, pl.ds(0, nwords)], own_sem.at[p]
            ).wait()
            pltpu.make_async_remote_copy(
                src_ref=unembed_hbm.at[:, columns(plane)],
                dst_ref=words.at[1, plane, pl.ds(0, nwords)],
                send_sem=words_send.at[p],
                recv_sem=words_recv.at[p],
                device_id=partner,
                device_id_type=MESH,
            ).wait_recv()

        for half in range(2):
            product = lax.dot_general(
                words[half, plane, 0:nwords, :], rows[...], (((1,), (1,)), ((), ())), preferred_element_type=F32
            )
            acc[half, 0:nwords, :] = jnp.where(p == 0, 0.0, acc[half, 0:nwords, :]) + product
            dispatch(s, [functools.partial(run, step[1 + half]) if step[1 + half] else None for step in PLAN])

        @pl.when(p == 3)
        def _():
            sums = jnp.sum(jnp.transpose(squares[...]), axis=0, keepdims=True)
            inverse = lax.rsqrt(sums / (4 * plane_width) + EPSILON)

            def top(i, most):
                start = pl.multiple_of(i * 200, 8)
                for half in range(2):
                    for k in range(25):
                        most = jnp.maximum(most, acc[half, pl.ds(start + 8 * k, 8), :])
                return most

            most = lax.fori_loop(0, 6, top, jnp.full((8, 256), FILL, F32))
            scale = jnp.broadcast_to(inverse, (8, 256))
            peak = jnp.max(most, axis=0, keepdims=True) * inverse
            peaks = jnp.broadcast_to(peak, (8, 256))
            target = targets_v[core * GROUPS + g]
            sublane = lax.broadcasted_iota(jnp.int32, (8, 256), 0)
            wanted = []
            for half in range(2):
                holder = core if half == 0 else 1 - core
                first_word = (((y * 2 + holder) * 4 + x) * 4 + z) * nwords
                local = target - first_word
                local = jnp.where(local < nwords, local, -8)
                wanted.append(jnp.broadcast_to(local, (8, 256)) - sublane)

            def fold(i, carry):
                mass, moment, picked = carry
                start = pl.multiple_of(i * 200, 8)
                for half in range(2):
                    for k in range(25):
                        z_all = acc[half, pl.ds(start + 8 * k, 8), :] * scale
                        z_rel = z_all - peaks
                        e = jnp.exp(z_rel)
                        mass = mass + e
                        moment = moment + e * z_rel
                        picked = jnp.where(wanted[half] == start + 8 * k, z_all, picked)
                return mass, moment, picked

            zero = jnp.zeros((8, 256), F32)
            mass, moment, picked = lax.fori_loop(0, 6, fold, (zero, zero, zero))
            found = [peak] + [jnp.sum(v, axis=0, keepdims=True) for v in (mass, moment, picked)]
            for k, value in enumerate(found):
                stats[g, 2 * k : 2 * k + 1, :] = value[:, 0:128]
                stats[g, 2 * k + 1 : 2 * k + 2, :] = value[:, 128:256]

        return carry

    lax.fori_loop(0, 4 * GROUPS, body, 0)

    def joined(parts):
        tops = [part[:, 0:2, :] for part in parts]
        most = functools.reduce(jnp.maximum, tops)
        shifts = [top - most for top in tops]
        factors = [jnp.exp(shift) for shift in shifts]
        mass = sum(f * part[:, 2:4, :] for f, part in zip(factors, parts))
        moment = sum(
            f * (part[:, 4:6, :] + shift * part[:, 2:4, :]) for f, shift, part in zip(factors, shifts, parts)
        )
        picked = sum(part[:, 6:8, :] for part in parts)
        return most, mass, moment, picked

    waits = []

    def exchanged(axis, mine, inbox, send, recv, result):
        copies = []
        for step in (1, 2, 3):
            copies.append(
                pltpu.make_async_remote_copy(
                    src_ref=mine,
                    dst_ref=inbox.at[step - 1],
                    send_sem=send.at[step - 1],
                    recv_sem=recv.at[step - 1],
                    device_id=device(*moved(axis, step), core),
                    device_id_type=MESH,
                )
            )
        for copy in copies:
            copy.start()
        for copy in copies:
            copy.wait_recv()
        waits.extend(copies)
        for k, value in enumerate(joined([mine[...]] + [inbox[k] for k in range(3)])):
            result[:, 2 * k : 2 * k + 2, :] = value

    exchanged(0, stats, from_x, x_send, x_recv, stats_x)
    exchanged(1, stats_x, from_y, y_send, y_recv, stats_y)

    def last_copy(step, other, towards):
        cc = 1 - core if other else core
        origin = core if towards else cc
        return pltpu.make_async_remote_copy(
            src_ref=stats_y,
            dst_ref=from_z.at[origin, step],
            send_sem=z_send.at[4 * other + step],
            recv_sem=z_recv.at[4 * other + step],
            device_id=device(*moved(2, step), cc),
            device_id_type=MESH,
        )

    lasts = [(1, True), (2, True), (3, True), (1, False), (2, False), (3, False), (0, True)]
    for step, other in lasts:
        last_copy(step, other, True).start()
    from_z[core, 0] = stats_y[...]
    for step, other in lasts:
        last_copy(step, other, False).wait_recv()
    for half in range(2):
        most, mass, moment, picked = joined([from_z[half, k] for k in range(4)])
        log_mass = jnp.log(mass)
        lse = most + log_mass
        out_ref[0, half] = lse
        out_ref[1, half] = log_mass - moment / mass
        out_ref[2, half] = picked - lse

    for step, other in lasts:
        last_copy(step, other, True).wait_send()
    for copy in waits:
        copy.wait_send()
    part.wait_send()
    for copy in their_words:
        copy.wait_send()
    for row, (dx, dy, dz, link) in enumerate(TREE):
        if dy == 0:
            gain_copy(parent((dx, dy, dz), link), link).wait_send()
    for g in range(GROUPS):
        pltpu.make_async_remote_copy(
            src_ref=gat.at[pl.ds(0, len(TREE))],
            dst_ref=gat.at[pl.ds(0, len(TREE))],
            send_sem=send_sem.at[g],
            recv_sem=recv_sem.at[0],
            device_id=neighbours[0],
            device_id_type=MESH,
        ).wait_send()


def wrapped(c):
    return (c + 1) % 4 - 1


def parent(n, link):
    axis, way = LINKS[link]
    n = list(n)
    n[axis] = wrapped(n[axis] - way)
    return tuple(n)


def child(n, link):
    axis, way = LINKS[link]
    n = list(n)
    n[axis] = wrapped(n[axis] + way)
    return tuple(n)


TREE_INDEX = {row[:3]: k for k, row in enumerate(TREE)}
GAIN_INDEX = {k: i for i, k in enumerate(k for k, row in enumerate(TREE) if row[1] == 0)}


def shards(stream_in, deltas, norm_gain, unembed, targets):
    nwords, width = unembed.shape
    odd = lax.rem(lax.axis_index("vocab_1"), 2) == 1
    gap = jnp.zeros((320,), F32)
    rest = jnp.zeros((384,), F32)
    gain = jnp.where(
        odd, jnp.concatenate([gap, norm_gain, rest]), jnp.concatenate([norm_gain, gap, rest])
    ).reshape(8, 128)
    wanted = jnp.broadcast_to(targets.reshape(8, 1, 1, GTOK), (8, 1, 16, GTOK)).reshape(8, 1, 256)
    anywhere = pl.BlockSpec(memory_space=pl.ANY)
    dma = pltpu.SemaphoreType.DMA
    out = pl.pallas_call(
        kernel,
        out_shape=jax.ShapeDtypeStruct((3, 2, GROUPS, 2, 128), F32),
        in_specs=[anywhere] * 5,
        out_specs=pl.BlockSpec(memory_space=pltpu.VMEM),
        scratch_shapes=[
            pltpu.VMEM((128, 320), BF16),
            pltpu.VMEM((2, 128, 320), BF16),
            pltpu.VMEM((8, 1, 256), jnp.int32),
            pltpu.VMEM((16, 8, 128), F32),
            pltpu.VMEM((GROUPS, 5, GTOK, 128), BF16),
            pltpu.VMEM((64 * GROUPS, 2, 5, GTOK, 128), BF16),
            pltpu.VMEM((2, 4, nwords, width // 4), BF16),
            pltpu.VMEM((256, width // 4), BF16),
            pltpu.VMEM((2, 1200, 256), F32),
            pltpu.VMEM((256, 128), F32),
            pltpu.VMEM((GROUPS, 8, 128), F32),
            pltpu.VMEM((3, GROUPS, 8, 128), F32),
            pltpu.VMEM((GROUPS, 8, 128), F32),
            pltpu.VMEM((3, GROUPS, 8, 128), F32),
            pltpu.VMEM((GROUPS, 8, 128), F32),
            pltpu.VMEM((2, 4, GROUPS, 8, 128), F32),
            dma((4,)),
            dma((4,)),
            dma((4,)),
            dma((4,)),
            dma((15,)),
            dma((15,)),
            dma,
            dma,
            dma((GROUPS,)),
            dma((63 * GROUPS,)),
            dma((3,)),
            dma((3,)),
            dma((3,)),
            dma((3,)),
            dma((8,)),
            dma((8,)),
        ],
        compiler_params=pltpu.CompilerParams(
            collective_id=0, has_side_effects=True, vmem_limit_bytes=60 * 1024 * 1024
        ),
    )(stream_in, deltas, gain, unembed, wanted)
    layers = out.reshape(3, 2, GROUPS, 16, GTOK).transpose(0, 3, 1, 2, 4).reshape(3, 16, 128)
    mine = lax.dynamic_slice_in_dim(layers, 2 * lax.axis_index("section"), 2, axis=1)
    return mine[0], mine[1], mine[2]


def solution(mesh):
    torus = Mesh(
        mesh.devices.reshape(mesh.shape["section"], 4, 4), ("section", "vocab_0", "vocab_1")
    )
    placed = (P(None, VOCAB), P("section", None, VOCAB), P(VOCAB), P(SECTION_VOCAB, None), P())
    return jax.shard_map(
        shards,
        mesh=torus,
        in_specs=placed,
        out_specs=(P("section", None), P("section", None), P("section", None)),
        check_vma=False,
    )
```

time: 258 us -> 120 us (0.47)
  waiting for transfers between devices: 122 us -> 0 us
  Pallas kernels: 0 us -> 111 us
  blocking collectives: 71.7 us -> 0 us
  matrix products: 30.1 us -> 0 us
  between operations: 14.2 us -> 0.69 us
  starting transfers between devices: 5.96 us -> 0 us
  other arithmetic: 7.33 us -> 1.42 us
    pallas_call x0 -> x1, Pallas kernels: none -> 111 us  [shards(): pl.pallas_call(kernel, out_shape=jax.ShapeDtypeStruct((3, 2, GROUPS, 2, 1...]
    all_gather x1 -> x0, waiting for transfers between devices: 104 us -> none  [shards(): lax.all_gather(features, 'section', axis=0, tiled=True)]
    all_to_all x3 -> x0, blocking collectives: 53.3 us -> none  [the longest x2 44.7 us: from_everyone(): lax.all_to_all(jnp.broadcast_to(value[None], (size, *value.shape)), axis,...]
    dot_general x1 -> x0, matrix products: 30.1 us -> none  [shards(): jnp.einsum('wd,ltd->lwt', unembed, lax.all_gather(features, 'section', ax...]
    psum x2 -> x0, blocking collectives: 18.4 us -> none  [over_axes(): return functools.reduce(lax.psum, axes, value)]
    all_to_all x1 -> x0, waiting for transfers between devices: 17.8 us -> none  [from_everyone(): lax.all_to_all(jnp.broadcast_to(value[None], (size, *value.shape)), axis,...]
    all_to_all x1 -> x0, starting transfers between devices: 5.96 us -> none  [from_everyone(): lax.all_to_all(jnp.broadcast_to(value[None], (size, *value.shape)), axis,...]
    unnamed x4 -> x2, local copies, waits for them, and re-layouts: 0.01 us -> 3.35 us
  transfers between devices with their start and end apart: 2 -> 0, of which waited for: 2 -> 0; matrix products, arithmetic and copies ran while one was open for 0% -> 0% of each run, Pallas kernels for 0% -> 0%
where the time goes in v1:
time: 120 us; the launch traced here: 119 us
  Pallas kernels  111 us (92%)
  local copies, waits for them, and re-layouts  6.46 us (5%)
  other arithmetic  1.42 us (1%)
    pallas_call x1, Pallas kernels, shards(): pl.pallas_call(kernel, out_shape=jax.ShapeDtypeStruct((3, 2, GROUPS, 2, 1...  111 us
    unnamed x2, local copies, waits for them, and re-layouts  3.35 us

profile of v1, /device:TPU:1, one launch (start us, length us, event | category | flops | bytes accessed | tf_op | source)
XLA Modules:
  0.0 119.4 jit_solution(16014271750428959992)
XLA Ops:
  0.7 1.4 %fusion.1.gain_hbm = f32[8,128]{1,0:T(8,128)} fusion(f32[384]{0:T(512)S(1)} %broadcast_in_dim.16, f32[320]{0:T(512)} %param.7, f32[320]{0:T(512)S(1)} %broadcast_in_dim.15, pred[]{:T(512)S(6)} %eq.3), kind=kLoop, calls=%fused_computation.3 | loop fusion | flops 5120 | bytes 8193 | tf_op jit(solution)/shard_map/jit(_where)/select_n | solution.py:651
  2.1 1.7 %copy.9.deltas_hbm = bf16[2,128,320]{2,1,0:T(8,128)(2,1)} copy(bf16[2,128,320]{1,2,0:T(8,128)(2,1)} %param.6) | data formatting | bytes 327680 | tf_op args[1]
  3.8 1.6 %copy.8.stream_hbm = bf16[128,320]{1,0:T(8,128)(2,1)} copy(bf16[128,320]{0,1:T(8,128)(2,1)} %param.5) | data formatting | bytes 163840 | tf_op args[0]
  5.4 0.7 broadcast_in_dim.17
  6.2 0.7 broadcast_in_dim.19.targets_hbm
  6.9 110.8 %shard_map.76 = f32[3,2,4,2,128]{4,3,2,1,0:T(2,128)} custom-call(bf16[128,320]{1,0:T(8,128)(2,1)} %copy.8.stream_hbm, bf16[2,128,320]{2,1,0:T(8,128)(2,1)} %copy.9.deltas_hbm, f32[8,128]{1,0:T(8,128)} %fusion.1.gain_hbm, bf16[1188,5120]{1,0:T(8,128)(2,1)} %unembed_hbm.1, s32[8,1,256]{2,1,0:T(1,128)} %broadcast_in_dim.19.targets_hbm), custom_call_target="tpu_custom_call" | custom-call | tf_op jit(solution)/shard_map/pallas_call | solution.py:657
  117.7 0.9 reshape.25
  118.6 0.1 copy.10
  118.6 0.2 reshape.26
  118.8 0.6 dynamic-slice_bitcast_fusion
  (3 shorter events, 0.0 us)

commit v2 on v1

v2 whole, which is shorter than its diff:
```python
import functools

import jax
import jax.numpy as jnp
from jax import lax
from jax.experimental import pallas as pl
from jax.experimental.pallas import tpu as pltpu
from jax.sharding import Mesh
from jax.sharding import PartitionSpec as P

MESH = pl.DeviceIdType.MESH
F32 = jnp.float32
BF16 = jnp.bfloat16
EPSILON = 1e-06

VOCAB = ("vocab_0", "vocab_1")
SECTION_VOCAB = ("section", "vocab_0", "vocab_1")

LINKS = ((0, 1), (0, -1), (1, 1), (1, -1), (2, 1), (2, -1))
TREE = (
    (-1, 0, 0, 1), (0, -1, 0, 3), (0, 0, -1, 5), (0, 0, 1, 4), (0, 1, 0, 2), (1, 0, 0, 0),
    (-1, -1, 0, 1), (-1, 0, -1, 1), (-1, 0, 1, 1), (-1, 1, 0, 1), (0, -1, -1, 3), (0, -1, 1, 3),
    (0, 0, 2, 5), (0, 1, -1, 5), (0, 1, 1, 4), (0, 2, 0, 2), (1, -1, 0, 0), (1, 0, -1, 0),
    (1, 0, 1, 0), (1, 1, 0, 0), (2, 0, 0, 1), (-1, -1, -1, 5), (-1, -1, 1, 3), (-1, 0, 2, 4),
    (-1, 1, -1, 1), (-1, 1, 1, 1), (-1, 2, 0, 3), (0, -1, 2, 4), (0, 1, 2, 4), (0, 2, -1, 3),
    (0, 2, 1, 2), (1, -1, -1, 5), (1, -1, 1, 3), (1, 0, 2, 5), (1, 1, -1, 5), (1, 1, 1, 4),
    (1, 2, 0, 3), (2, -1, 0, 0), (2, 0, -1, 0), (2, 0, 1, 0), (2, 1, 0, 1), (-1, -1, 2, 5),
    (-1, 1, 2, 2), (-1, 2, -1, 2), (-1, 2, 1, 3), (0, 2, 2, 2), (1, -1, 2, 0), (1, 1, 2, 5),
    (1, 2, -1, 5), (1, 2, 1, 2), (2, -1, -1, 3), (2, -1, 1, 0), (2, 0, 2, 1), (2, 1, -1, 5),
    (2, 1, 1, 1), (2, 2, 0, 2), (-1, 2, 2, 2), (1, 2, 2, 4), (2, -1, 2, 3), (2, 1, 2, 2),
    (2, 2, -1, 2), (2, 2, 1, 0), (2, 2, 2, 4),
)
PLAN = (
    (
        (1, 0, 0), (1, 1, 0), (1, 2, 0), (1, 3, 0), (1, 4, 0), (1, 5, 0), (1, 0, 1), (1, 1, 1), (1, 2, 1),
        (1, 3, 1), (1, 4, 1), (1, 5, 1), (1, 0, 2), (1, 1, 2), (1, 2, 2), (1, 3, 2), (1, 4, 2), (1, 5, 2),
        (1, 0, 3), (1, 1, 3), (1, 2, 3), (1, 3, 3), (1, 4, 3), (1, 5, 3), (0, 0, 0), (0, 1, 0), (0, 2, 0),
        (0, 3, 0), (0, 4, 0), (0, 5, 0), (1, 9, 0), (1, 11, 0), (1, 13, 0), (1, 14, 0), (1, 15, 0), (1, 19, 0),
        (1, 8, 0), (1, 10, 0), (0, 0, 1), (0, 1, 1), (0, 2, 1), (0, 3, 1), (0, 4, 1), (0, 5, 1), (1, 13, 1),
        (1, 14, 1), (1, 15, 1), (1, 19, 1), (1, 6, 0), (1, 11, 1), (1, 12, 0), (1, 16, 0), (0, 0, 2), (0, 1, 2),
        (0, 2, 2), (0, 3, 2), (0, 4, 2), (0, 5, 2), (1, 14, 2), (1, 15, 2), (1, 9, 1), (1, 10, 1), (1, 13, 2),
        (1, 18, 0), (0, 0, 3), (0, 1, 3), (0, 2, 3), (0, 3, 3), (0, 4, 3), (0, 5, 3), (1, 14, 3), (1, 15, 3),
        (1, 8, 1), (1, 11, 2), (1, 12, 1), (1, 17, 0), (0, 9, 0), (0, 11, 0), (0, 13, 0), (0, 14, 0), (0, 15, 0),
        (0, 19, 0), (1, 30, 0), (1, 35, 0), (1, 10, 2), (1, 34, 0), (1, 19, 2), (1, 40, 0), (0, 8, 0), (0, 10, 0),
        (0, 13, 1), (0, 14, 1), (0, 15, 1), (0, 19, 1), (1, 23, 0), (1, 30, 1), (1, 22, 0), (1, 24, 0), (1, 16, 1),
        (1, 34, 1), (1, 35, 1), (0, 6, 0), (0, 11, 1), (0, 12, 0), (0, 14, 2), (0, 15, 2), (0, 16, 0), (1, 30, 2),
        (1, 21, 0), (1, 25, 0), (1, 18, 1), (1, 36, 0), (1, 27, 0), (0, 9, 1), (0, 10, 1), (0, 13, 2), (0, 14, 3),
        (0, 15, 3), (0, 18, 0), (1, 30, 3), (1, 31, 0), (1, 32, 0), (1, 17, 1), (1, 40, 1), (1, 28, 0), (0, 8, 1),
        (0, 11, 2), (0, 12, 1), (0, 17, 0), (1, 6, 1), (1, 29, 0), (1, 33, 0), (1, 38, 0), (0, 30, 0), (0, 35, 0),
        (1, 49, 0), (1, 23, 1), (0, 10, 2), (0, 34, 0), (0, 19, 2), (0, 40, 0), (1, 26, 0), (1, 19, 3), (1, 53, 0),
        (0, 23, 0), (0, 30, 1), (1, 42, 0), (1, 52, 0), (1, 35, 2), (0, 22, 0), (0, 24, 0), (0, 16, 1), (0, 34, 1),
        (1, 9, 2), (1, 44, 0), (1, 47, 0), (1, 39, 0), (0, 30, 2), (0, 35, 1), (1, 49, 1), (1, 27, 1), (1, 55, 0),
        (0, 21, 0), (0, 25, 0), (0, 18, 1), (0, 36, 0), (1, 41, 0), (1, 8, 2), (1, 36, 1), (0, 27, 0), (0, 30, 3),
        (1, 46, 0), (1, 28, 1), (0, 31, 0), (0, 32, 0), (0, 17, 1), (0, 40, 1), (1, 32, 1), (1, 48, 0), (1, 20, 0),
        (0, 28, 0), (1, 45, 0), (0, 49, 0), (1, 57, 0), (1, 61, 0), (1, 43, 0), (0, 6, 1), (0, 29, 0), (0, 33, 0),
        (0, 38, 0), (1, 7, 0), (1, 50, 0), (1, 51, 0), (1, 53, 1), (0, 23, 1), (0, 42, 0), (1, 56, 0), (0, 26, 0),
        (0, 19, 3), (0, 52, 0), (0, 53, 0), (1, 35, 3), (1, 21, 1), (1, 58, 0), (1, 38, 1), (1, 54, 0), (0, 35, 2),
        (0, 49, 1), (1, 57, 1), (1, 59, 0), (0, 9, 2), (0, 44, 0), (0, 47, 0), (0, 39, 0), (1, 22, 1), (1, 24, 1),
        (1, 31, 1), (1, 37, 0), (0, 27, 1), (0, 55, 0), (1, 60, 0), (0, 41, 0), (0, 8, 2), (0, 46, 0), (0, 36, 1),
        (1, 23, 2), (1, 29, 1), (1, 48, 1), (1, 52, 1), (1, 61, 1), (0, 28, 1), (0, 45, 0),
    ),
    (
        (1, 49, 2), (0, 32, 1), (0, 48, 0), (0, 20, 0), (0, 61, 0), (1, 62, 0), (1, 25, 1), (1, 26, 1), (1, 16, 2),
        (1, 47, 1), (0, 57, 0),
    ),
    (
        (1, 27, 2), (0, 43, 0), (1, 42, 1), (0, 7, 0), (0, 50, 0), (0, 51, 0), (0, 53, 1), (1, 22, 2), (1, 18, 2),
        (1, 33, 1), (1, 40, 2),
    ),
    (
        (0, 35, 3), (1, 28, 2), (0, 56, 0), (1, 45, 1), (0, 21, 1), (0, 58, 0), (0, 38, 1), (0, 54, 0), (1, 6, 2),
        (1, 41, 1), (1, 17, 2), (1, 50, 1),
    ),
    (
        (0, 57, 1), (1, 28, 3), (0, 59, 0), (1, 55, 1), (0, 22, 1), (0, 24, 1), (0, 31, 1), (0, 37, 0), (1, 9, 3),
        (1, 44, 1), (1, 46, 1), (1, 34, 2),
    ),
    (
        (0, 23, 2), (0, 60, 0), (0, 29, 1), (0, 48, 1), (0, 52, 1), (0, 61, 1), (1, 59, 1), (1, 62, 1), (1, 8, 3),
        (1, 13, 3), (1, 51, 1), (1, 58, 1), (0, 62, 0),
    ),
    (
        (0, 49, 2), (1, 57, 2), (1, 43, 1), (0, 25, 1), (0, 26, 1), (0, 16, 2), (0, 47, 1), (1, 31, 2), (1, 36, 2),
        (1, 20, 1), (1, 39, 1),
    ),
    (
        (0, 27, 2), (0, 42, 1), (1, 56, 1), (0, 22, 2), (0, 18, 2), (0, 33, 1), (0, 40, 2), (1, 7, 1), (1, 32, 2),
        (1, 37, 1), (1, 53, 2), (0, 28, 2), (0, 45, 1),
    ),
    (
        (1, 60, 1), (0, 6, 2), (0, 41, 1), (0, 17, 2), (0, 50, 1), (1, 21, 2), (1, 11, 3), (1, 38, 2), (1, 54, 1),
        (0, 28, 3),
    ),
    (
        (0, 55, 1), (1, 49, 3), (0, 9, 3), (0, 44, 1), (0, 46, 1), (0, 34, 2), (1, 24, 2), (1, 44, 2), (1, 12, 2),
        (1, 61, 2), (0, 62, 1),
    ),
    (
        (0, 59, 1), (1, 42, 2), (0, 8, 3), (0, 13, 3), (0, 51, 1), (0, 58, 1), (1, 23, 3), (1, 29, 2), (1, 16, 3),
        (1, 47, 2), (1, 52, 2), (0, 57, 2),
    ),
    (
        (0, 43, 1), (1, 45, 2), (0, 31, 2), (0, 36, 2), (0, 20, 1), (0, 39, 1), (1, 25, 2), (1, 26, 2), (1, 18, 3),
        (1, 48, 2), (0, 56, 1), (1, 55, 2), (0, 7, 1), (0, 32, 2), (0, 37, 1), (0, 53, 2),
    ),
    (
        (1, 10, 3), (1, 17, 3), (1, 33, 2), (1, 40, 3), (0, 60, 1), (1, 60, 2),
    ),
    (
        (0, 21, 2), (0, 11, 3), (0, 38, 2), (0, 54, 1), (1, 27, 3), (1, 6, 3), (1, 41, 2), (1, 46, 2), (1, 50, 2),
        (0, 49, 3),
    ),
    (
        (0, 24, 2), (0, 44, 2), (0, 12, 2), (0, 61, 2), (1, 43, 2), (1, 62, 2), (1, 22, 3), (1, 34, 3), (1, 51, 2),
        (1, 20, 2), (0, 23, 3), (1, 57, 3), (0, 42, 2), (1, 56, 2),
    ),
    (
        (0, 29, 2), (0, 16, 3), (0, 47, 2), (0, 52, 2), (1, 7, 2), (1, 31, 3), (1, 58, 2), (1, 39, 2), (0, 45, 2),
        (1, 59, 2),
    ),
    (
        (0, 25, 2), (0, 26, 2), (0, 18, 3), (0, 48, 2), (1, 12, 3), (1, 36, 3), (1, 37, 2), (1, 54, 2), (0, 55, 2),
        (1, 42, 3),
    ),
    (
        (0, 10, 3), (0, 17, 3), (0, 33, 2), (0, 40, 3), (1, 24, 3), (1, 32, 3), (1, 38, 3), (1, 53, 3), (0, 27, 3),
        (0, 60, 2), (1, 45, 3), (0, 6, 3), (0, 41, 2), (0, 46, 2), (0, 50, 2),
    ),
    (
        (1, 21, 3), (1, 29, 3), (1, 52, 3), (1, 61, 3), (0, 62, 2), (0, 43, 2), (1, 55, 3),
    ),
    (
        (0, 22, 3), (0, 34, 3), (0, 51, 2), (0, 20, 2), (1, 25, 3), (1, 44, 3), (1, 46, 3), (1, 47, 3), (0, 57, 3),
        (0, 56, 2), (0, 7, 2), (0, 31, 3), (0, 58, 2), (0, 39, 2),
    ),
    (
        (1, 26, 3), (1, 33, 3), (1, 20, 3), (1, 39, 3), (0, 59, 2),
    ),
    (
        (0, 12, 3), (0, 36, 3), (0, 37, 2), (0, 54, 2), (1, 7, 3), (1, 48, 3), (1, 37, 3), (0, 42, 3), (1, 56, 3),
    ),
    (
        (0, 24, 3), (0, 32, 3), (0, 38, 3), (0, 53, 3), (1, 43, 3), (1, 50, 3), (1, 51, 3), (0, 45, 3),
    ),
    (
        (0, 21, 3), (0, 29, 3), (0, 52, 3), (0, 61, 3), (1, 41, 3), (1, 58, 3), (1, 59, 3), (1, 62, 3), (0, 55, 3),
        (1, 60, 3),
    ),
    (
        (0, 25, 3), (0, 44, 3), (0, 46, 3), (0, 47, 3), (1, 54, 3),
    ),
    (
        (0, 26, 3), (0, 33, 3), (0, 20, 3), (0, 39, 3), (0, 56, 3), (0, 7, 3), (0, 48, 3), (0, 37, 3),
    ),
    (
        (0, 50, 3), (0, 43, 3),
    ),
    (
        (0, 51, 3), (0, 41, 3), (0, 58, 3), (0, 62, 3), (0, 59, 3),
    ),
    (
        (0, 54, 3), (0, 60, 3),
    ),
    (),
    (),
    (),
    (),
    (),
)
PLANES = (0, 1, -1, 2)

GROUPS = 4
GTOK = 16
FILL = -1e30


def dispatch(index, branches, low=0, high=None):
    high = len(branches) if high is None else high
    if not any(branches[low:high]):
        return
    if high - low == 1:
        branches[low]()
        return
    mid = (low + high) // 2

    @pl.when(index < mid)
    def _():
        dispatch(index, branches, low, mid)

    @pl.when(index >= mid)
    def _():
        dispatch(index, branches, mid, high)


def kernel(
    stream_hbm, deltas_hbm, gain_hbm, unembed_hbm, targets_hbm, lse_ref, entropy_ref, logprob_ref,
    stream_v, deltas_v, targets_v, gain_v, gains, outbox, gat, words, rows_a, rows_b, acc, final,
    squares, scales, tops, sums, stats, from_x, stats_x, from_y, stats_y, from_z,
    load_sem, own_sem, words_send, words_recv, gain_send, gain_recv,
    part_send, part_recv, send_sem, recv_sem,
    x_send, x_recv, y_send, y_recv, z_send, z_recv,
):
    section = lax.axis_index("section")
    x = lax.axis_index("vocab_0")
    z = lax.axis_index("vocab_1")
    y = section // 2
    core = section % 2
    sign = 1 - 2 * core
    nwords = unembed_hbm.shape[0]
    plane_width = unembed_hbm.shape[1] // 4
    home = (x, y, z)

    def device(xx, yy, zz, cc):
        return (yy * 2 + cc, xx, zz)

    def moved(axis, step):
        at = list(home)
        at[axis] = lax.rem(at[axis] + step + 4, 4)
        return tuple(at)

    neighbours = [device(*moved(axis, way * sign), core) for axis, way in LINKS]
    partner = device(x, y, z, 1 - core)
    source = [{d: lax.rem(home[axis] - sign * d + 4, 4) for d in (-1, 0, 1, 2)} for axis in range(3)]

    loads = [
        pltpu.make_async_copy(stream_hbm, stream_v, load_sem.at[0]),
        pltpu.make_async_copy(deltas_hbm, deltas_v, load_sem.at[1]),
        pltpu.make_async_copy(targets_hbm, targets_v, load_sem.at[2]),
        pltpu.make_async_copy(gain_hbm, gain_v, load_sem.at[3]),
    ]
    for copy in loads:
        copy.start()

    barrier = pltpu.get_barrier_semaphore()
    for axis in range(3):
        for step in (1, 2, 3):
            at = moved(axis, step)
            pl.semaphore_signal(barrier, inc=1, device_id=device(*at, core), device_id_type=MESH)
            if axis == 2:
                pl.semaphore_signal(barrier, inc=1, device_id=device(*at, 1 - core), device_id_type=MESH)
    pl.semaphore_signal(barrier, inc=1, device_id=partner, device_id_type=MESH)

    def columns(plane):
        return pl.ds(pl.multiple_of(plane * plane_width, 128), plane_width)

    own_words = []
    for p, dx in enumerate(PLANES):
        plane = source[0][dx]
        own_words.append(
            pltpu.make_async_copy(
                unembed_hbm.at[:, columns(plane)], words.at[0, plane, pl.ds(0, nwords)], own_sem.at[p]
            )
        )
        own_words[-1].start()

    for copy in loads:
        copy.wait()

    lane = lax.broadcasted_iota(jnp.int32, (GTOK, 128), 1)
    low = lane < 64
    odd = lax.rem(z, 2) == 1
    my_slot = ((x * 4 + y) * 4 + z) * GROUPS

    first = jnp.where(section == 0, 1.0, 0.0).astype(F32)
    former = deltas_v[0].astype(F32) + stream_v[...].astype(F32) * first
    kept = former.astype(BF16).astype(F32)
    latter = deltas_v[1].astype(F32) + (former - kept)
    packed = []
    heads = []
    for value in (kept, latter):
        packed.append(jnp.where(odd, value[64:192], value[0:128]))
        packed.append(jnp.where(odd, value[192:320], value[128:256]))
        heads.append(jnp.where(odd, value[0:64], value[256:320]))
    lead = jnp.where(odd, heads[1], heads[0])
    trail = jnp.where(odd, heads[0], heads[1])
    packed.append(jnp.concatenate([lead, trail], axis=0))
    for k, value in enumerate(packed):
        tile = jnp.transpose(value).astype(BF16)
        for half in range(2):

            @pl.when(core == half)
            def _():
                for g in range(GROUPS):
                    t0 = half * 64 + g * GTOK
                    gat[my_slot + g, core, k] = tile[t0 : t0 + GTOK]

            @pl.when(core != half)
            def _():
                for g in range(GROUPS):
                    t0 = half * 64 + g * GTOK
                    outbox[g, k] = tile[t0 : t0 + GTOK]

    low_row = lax.broadcasted_iota(jnp.int32, (1, 128), 1) < 64
    none = jnp.zeros((1, 64), F32)
    g0 = gain_v[0:128].reshape(1, 128)
    g1 = gain_v[128:256].reshape(1, 128)
    g2 = jnp.concatenate([gain_v[256:320].reshape(1, 64), none], axis=1)
    t0, t1, t2 = (pltpu.roll(v, 64, 1) for v in (g0, g1, g2))
    blank = jnp.zeros((1, 128), F32)
    gain_rows = (
        (g0, blank),
        (g1, blank),
        (g2, jnp.where(low_row, 0.0, t0)),
        (blank, jnp.where(low_row, t0, t1)),
        (blank, jnp.where(low_row, t1, t2)),
    )
    gains[x * 4 + z] = jnp.concatenate(
        [jnp.where(odd, other, even) for even, other in gain_rows] + [blank] * 3, axis=0
    )

    final[:, 1184:1200, :] = jnp.full((2, 16, 256), FILL, F32)

    pl.semaphore_wait(barrier, 13)

    part = pltpu.make_async_remote_copy(
        src_ref=outbox,
        dst_ref=gat.at[pl.ds(my_slot, GROUPS), core],
        send_sem=part_send,
        recv_sem=part_recv,
        device_id=partner,
        device_id_type=MESH,
    )
    part.start()

    def gain_copy(n, link):
        at = (source[0][n[0]] * 4 + source[2][n[2]])
        place = (TREE_INDEX[child(n, link)] if link is not None else TREE_INDEX[n])
        return pltpu.make_async_remote_copy(
            src_ref=gains.at[at],
            dst_ref=gains.at[at],
            send_sem=gain_send.at[GAIN_INDEX[place]],
            recv_sem=gain_recv.at[GAIN_INDEX[place]],
            device_id=neighbours[link or 0],
            device_id_type=MESH,
        )

    def block_copy(n, row, link, g):
        slot = source[0][n[0]] * 64 + source[1][n[1]] * 16 + source[2][n[2]] * 4 + g
        return pltpu.make_async_remote_copy(
            src_ref=gat.at[slot],
            dst_ref=gat.at[slot],
            send_sem=send_sem.at[g],
            recv_sem=recv_sem.at[row * GROUPS + g],
            device_id=neighbours[link],
            device_id_type=MESH,
        )

    def send_gain(n):
        for row, (dx, dy, dz, link) in enumerate(TREE):
            if dy == 0 and parent((dx, dy, dz), link) == n:
                gain_copy(n, link).start()

    def run(actions):
        for kind, row, g in actions:
            dx, dy, dz, link = TREE[row]
            n = (dx, dy, dz)
            if kind == 0:
                block_copy(n, row, link, g).wait_recv()
                if g == 0 and dy == 0:
                    gain_copy(n, None).wait_recv()
                    send_gain(n)
            else:
                block_copy(parent(n, link), row, link, g).start()

    send_gain((0, 0, 0))

    their_words = []
    for p, dx in enumerate(PLANES):
        plane = lax.rem(x + sign * dx + 4, 4)
        their_words.append(
            pltpu.make_async_remote_copy(
                src_ref=unembed_hbm.at[:, columns(plane)],
                dst_ref=words.at[1, plane, pl.ds(0, nwords)],
                send_sem=words_send.at[p],
                recv_sem=words_recv.at[p],
                device_id=partner,
                device_id_type=MESH,
            )
        )

    for copy in their_words:
        copy.start()
    part.wait_recv()

    segment = lax.broadcasted_iota(jnp.int32, (1, 128), 1) // GTOK

    def spread(value):
        for step in (16, 32, 64):
            value = value + pltpu.roll(value, step, 1)
        return value

    def prepare(g, p, zp, rows):
        plane = source[0][PLANES[p]]
        running = [jnp.zeros((GTOK, 128), F32) for _ in range(5)]
        both = gains[plane * 4 + 2 * zp] + gains[plane * 4 + 2 * zp + 1]
        factor = [jnp.broadcast_to(both[k : k + 1, :], (GTOK, 128)) for k in range(5)]
        for yy in range(4):
            even = plane * 64 + yy * 16 + 2 * zp * 4 + g
            other = even + 4
            for cc in range(2):
                pe = gat[even, cc, 4].astype(F32)
                po = gat[other, cc, 4].astype(F32)
                for l in range(2):
                    layer = 4 * yy + 2 * cc + l
                    if l == 0:
                        middle = jnp.where(low, pe, po)
                    else:
                        middle = pltpu.roll(jnp.where(low, po, pe), 64, 1)
                    values = [
                        gat[even, cc, 2 * l].astype(F32),
                        gat[even, cc, 2 * l + 1].astype(F32),
                        middle,
                        gat[other, cc, 2 * l].astype(F32),
                        gat[other, cc, 2 * l + 1].astype(F32),
                    ]
                    span = slice(layer * GTOK, (layer + 1) * GTOK)
                    total = jnp.zeros((GTOK, 128), F32) if p == 0 and zp == 0 else squares[span, :]
                    for k in range(5):
                        at = 5 * zp + k
                        running[k] = running[k] + values[k]
                        total = total + running[k] * running[k]
                        rows[span, at * 128 : (at + 1) * 128] = (running[k] * factor[k]).astype(BF16)
                    squares[span, :] = total

    def multiply(p, stretch, rows):
        start, stop = ((0, 592), (592, nwords))[stretch]
        plane = source[0][PLANES[p]]
        most = []
        for half in range(2):
            product = lax.dot_general(
                words[half, plane, start:stop, :], rows[...], (((1,), (1,)), ((), ())), preferred_element_type=F32
            )
            if p == 0:
                acc[half, start:stop, :] = product
            elif p < 3:
                acc[half, start:stop, :] = acc[half, start:stop, :] + product
            else:
                total = acc[half, start:stop, :] + product
                final[half, start:stop, :] = total
                most.append(jnp.max(total[0:592].reshape(74, 8, 256), axis=0))
                if stop - start > 592:
                    most.append(jnp.broadcast_to(jnp.max(total[592:], axis=0, keepdims=True), (8, 256)))
        if p == 3:
            if stretch == 1:
                most.append(tops[...])
            tops[...] = functools.reduce(jnp.maximum, most)

    def scaled():
        total = jnp.sum(jnp.transpose(squares[...]), axis=0, keepdims=True)
        scales[0:1, :] = lax.rsqrt(total / (4 * plane_width) + EPSILON)

    def peaked():
        scales[1:2, :] = jnp.max(tops[...], axis=0, keepdims=True) * scales[0:1, :]

    def folded(g, half):
        scale = jnp.broadcast_to(scales[0:1, :], (8, 256))
        peaks = jnp.broadcast_to(scales[1:2, :], (8, 256))
        sublane = lax.broadcasted_iota(jnp.int32, (8, 256), 0)
        holder = core if half == 0 else 1 - core
        first_word = (((y * 2 + holder) * 4 + x) * 4 + z) * nwords
        local = targets_v[...].reshape(1, 128) - first_word
        local = jnp.where(local < nwords, local, -8)
        local = spread(jnp.where(segment == core * GROUPS + g, local, 0))
        wanted = jnp.broadcast_to(jnp.concatenate([local, local], axis=1), (8, 256)) - sublane
        if half == 0:
            mass = moment = picked = jnp.zeros((8, 256), F32)
        else:
            mass, moment, picked = (sums[k] for k in range(3))
        for k in range(150):
            z_all = final[half, 8 * k : 8 * k + 8, :] * scale
            z_rel = z_all - peaks
            e = jnp.exp(z_rel)
            mass = mass + e
            moment = moment + e * z_rel
            picked = jnp.where(wanted == 8 * k, z_all, picked)
        if half == 0:
            for k, value in enumerate((mass, moment, picked)):
                sums[k] = value
            return
        found = [scales[1:2, :]] + [jnp.sum(v, axis=0, keepdims=True) for v in (mass, moment, picked)]
        for k, value in enumerate(found):
            stats[g, 2 * k : 2 * k + 1, :] = value[:, 0:128]
            stats[g, 2 * k + 1 : 2 * k + 2, :] = value[:, 128:256]

    def place(p, k, g):
        dispatch(g, [functools.partial(run, PLAN[1 + 2 * (4 * j + p) + k]) if PLAN[1 + 2 * (4 * j + p) + k] else None for j in range(GROUPS)])

    run(PLAN[0])
    for zp in range(2):
        prepare(0, 0, zp, rows_a)

    def body(g, carry):
        for p in range(4):
            now, later = (rows_a, rows_b) if p % 2 == 0 else (rows_b, rows_a)
            following = (g, p + 1) if p < 3 else (jnp.minimum(g + 1, GROUPS - 1), 0)
            former_group = lax.rem(g + GROUPS - 1, GROUPS)
            place(p, 0, g)

            @pl.when(g == 0)
            def _():
                plane = source[0][PLANES[p]]
                own_words[p].wait()
                pltpu.make_async_remote_copy(
                    src_ref=unembed_hbm.at[:, columns(plane)],
                    dst_ref=words.at[1, plane, pl.ds(0, nwords)],
                    send_sem=words_send.at[p],
                    recv_sem=words_recv.at[p],
                    device_id=partner,
                    device_id_type=MESH,
                ).wait_recv()

            if p == 3:
                scaled()
            for k in range(2):
                if k == 1:
                    place(p, 1, g)
                multiply(p, k, now)
                prepare(*following, k, later)
                if p == 0:
                    folded(former_group, k)
            if p == 3:
                peaked()
        return carry

    lax.fori_loop(0, GROUPS, body, 0)
    run(PLAN[33])
    for half in range(2):
        folded(GROUPS - 1, half)

    def joined(parts):
        tops = [part[:, 0:2, :] for part in parts]
        most = functools.reduce(jnp.maximum, tops)
        shifts = [top - most for top in tops]
        factors = [jnp.exp(shift) for shift in shifts]
        mass = sum(f * part[:, 2:4, :] for f, part in zip(factors, parts))
        moment = sum(
            f * (part[:, 4:6, :] + shift * part[:, 2:4, :]) for f, shift, part in zip(factors, shifts, parts)
        )
        picked = sum(part[:, 6:8, :] for part in parts)
        return most, mass, moment, picked

    waits = []

    def exchanged(axis, mine, inbox, send, recv, result):
        copies = []
        for step in (1, 2, 3):
            copies.append(
                pltpu.make_async_remote_copy(
                    src_ref=mine,
                    dst_ref=inbox.at[step - 1],
                    send_sem=send.at[step - 1],
                    recv_sem=recv.at[step - 1],
                    device_id=device(*moved(axis, step), core),
                    device_id_type=MESH,
                )
            )
        for copy in copies:
            copy.start()
        for copy in copies:
            copy.wait_recv()
        waits.extend(copies)
        for k, value in enumerate(joined([mine[...]] + [inbox[k] for k in range(3)])):
            result[:, 2 * k : 2 * k + 2, :] = value

    exchanged(0, stats, from_x, x_send, x_recv, stats_x)
    exchanged(1, stats_x, from_y, y_send, y_recv, stats_y)

    def last_copy(step, other, towards):
        cc = 1 - core if other else core
        origin = core if towards else cc
        return pltpu.make_async_remote_copy(
            src_ref=stats_y,
            dst_ref=from_z.at[origin, step],
            send_sem=z_send.at[4 * other + step],
            recv_sem=z_recv.at[4 * other + step],
            device_id=device(*moved(2, step), cc),
            device_id_type=MESH,
        )

    lasts = [(1, True), (2, True), (3, True), (1, False), (2, False), (3, False), (0, True)]
    for step, other in lasts:
        last_copy(step, other, True).start()
    from_z[core, 0] = stats_y[...]
    for step, other in lasts:
        last_copy(step, other, False).wait_recv()
    found = [[], [], []]
    for half in range(2):
        most, mass, moment, picked = joined([from_z[half, k] for k in range(4)])
        log_mass = jnp.log(mass)
        lse = most + log_mass
        for k, value in enumerate((lse, log_mass - moment / mass, picked - lse)):
            found[k].append(jnp.where(y < 2, value[:, 0, :], value[:, 1, :]))
    grid_segment = lax.broadcasted_iota(jnp.int32, (8, 128), 1) // GTOK
    grid_row = lax.broadcasted_iota(jnp.int32, (8, 128), 0)
    for parts, out_ref in zip(found, (lse_ref, entropy_ref, logprob_ref)):
        grid = jnp.concatenate(parts, axis=0)
        for l in range(2):
            layer = lax.rem(4 * y + 2 * core, 8) + l
            value = spread(jnp.where(grid_segment == layer, grid, 0.0))
            out_ref[l : l + 1, :] = jnp.sum(jnp.where(grid_segment == grid_row, value, 0.0), axis=0, keepdims=True)

    for step, other in lasts:
        last_copy(step, other, True).wait_send()
    for copy in waits:
        copy.wait_send()
    part.wait_send()
    for copy in their_words:
        copy.wait_send()
    for row, (dx, dy, dz, link) in enumerate(TREE):
        if dy == 0:
            gain_copy(parent((dx, dy, dz), link), link).wait_send()
    for g in range(GROUPS):
        pltpu.make_async_remote_copy(
            src_ref=gat.at[pl.ds(0, len(TREE))],
            dst_ref=gat.at[pl.ds(0, len(TREE))],
            send_sem=send_sem.at[g],
            recv_sem=recv_sem.at[0],
            device_id=neighbours[0],
            device_id_type=MESH,
        ).wait_send()


def wrapped(c):
    return (c + 1) % 4 - 1


def parent(n, link):
    axis, way = LINKS[link]
    n = list(n)
    n[axis] = wrapped(n[axis] - way)
    return tuple(n)


def child(n, link):
    axis, way = LINKS[link]
    n = list(n)
    n[axis] = wrapped(n[axis] + way)
    return tuple(n)


TREE_INDEX = {row[:3]: k for k, row in enumerate(TREE)}
GAIN_INDEX = {k: i for i, k in enumerate(k for k, row in enumerate(TREE) if row[1] == 0)}


def shards(stream_in, deltas, norm_gain, unembed, targets):
    nwords, width = unembed.shape
    anywhere = pl.BlockSpec(memory_space=pl.ANY)
    inside = pl.BlockSpec(memory_space=pltpu.VMEM)
    dma = pltpu.SemaphoreType.DMA
    return pl.pallas_call(
        kernel,
        out_shape=(jax.ShapeDtypeStruct((2, 128), F32),) * 3,
        in_specs=[anywhere] * 5,
        out_specs=(inside,) * 3,
        scratch_shapes=[
            pltpu.VMEM((320, 128), BF16),
            pltpu.VMEM((2, 320, 128), BF16),
            pltpu.VMEM((128,), jnp.int32),
            pltpu.VMEM((320,), F32),
            pltpu.VMEM((16, 8, 128), F32),
            pltpu.VMEM((GROUPS, 5, GTOK, 128), BF16),
            pltpu.VMEM((64 * GROUPS, 2, 5, GTOK, 128), BF16),
            pltpu.VMEM((2, 4, nwords, width // 4), BF16),
            pltpu.VMEM((256, width // 4), BF16),
            pltpu.VMEM((256, width // 4), BF16),
            pltpu.VMEM((2, 1200, 256), F32),
            pltpu.VMEM((2, 1200, 256), F32),
            pltpu.VMEM((256, 128), F32),
            pltpu.VMEM((8, 256), F32),
            pltpu.VMEM((8, 256), F32),
            pltpu.VMEM((3, 8, 256), F32),
            pltpu.VMEM((GROUPS, 8, 128), F32),
            pltpu.VMEM((3, GROUPS, 8, 128), F32),
            pltpu.VMEM((GROUPS, 8, 128), F32),
            pltpu.VMEM((3, GROUPS, 8, 128), F32),
            pltpu.VMEM((GROUPS, 8, 128), F32),
            pltpu.VMEM((2, 4, GROUPS, 8, 128), F32),
            dma((4,)),
            dma((4,)),
            dma((4,)),
            dma((4,)),
            dma((15,)),
            dma((15,)),
            dma,
            dma,
            dma((GROUPS,)),
            dma((63 * GROUPS,)),
            dma((3,)),
            dma((3,)),
            dma((3,)),
            dma((3,)),
            dma((8,)),
            dma((8,)),
        ],
        compiler_params=pltpu.CompilerParams(
            collective_id=0, has_side_effects=True, vmem_limit_bytes=60 * 1024 * 1024
        ),
    )(stream_in.T, deltas.transpose(0, 2, 1), norm_gain, unembed, targets)


def solution(mesh):
    torus = Mesh(
        mesh.devices.reshape(mesh.shape["section"], 4, 4), ("section", "vocab_0", "vocab_1")
    )
    placed = (P(None, VOCAB), P("section", None, VOCAB), P(VOCAB), P(SECTION_VOCAB, None), P())
    return jax.shard_map(
        shards,
        mesh=torus,
        in_specs=placed,
        out_specs=(P("section", None), P("section", None), P("section", None)),
        check_vma=False,
    )
```

time: 120 us -> 86.6 us (0.72)
  Pallas kernels: 111 us -> 82.1 us
  local copies, waits for them, and re-layouts: 6.46 us -> 3.67 us
  other arithmetic: 1.42 us -> 0 us
    pallas_call x1, Pallas kernels: 111 us -> 82.1 us  [shards(): pl.pallas_call(kernel, out_shape=(jax.ShapeDtypeStruct((2, 128), F32),) *...]
    broadcast_in_dim x5 -> x0, local copies, waits for them, and re-layouts: 1.44 us -> none  [the longest x3 1.43 us: shards(): jnp.broadcast_to(targets.reshape(8, 1, 1, GTOK), (8, 1, 16, GTOK))]
    select_n x1 -> x0, other arithmetic: 1.42 us -> none  [shards(): jnp.where(odd, jnp.concatenate([gap, norm_gain, rest]), jnp.concatenate([...]
    unnamed x2 -> x3, local copies, waits for them, and re-layouts: 3.35 us -> 3.67 us
where the time goes in v2:
time: 86.6 us; the launch traced here: 86.4 us
  Pallas kernels  82.1 us (95%)
  local copies, waits for them, and re-layouts  3.67 us (4%)
    pallas_call x1, Pallas kernels, shards(): pl.pallas_call(kernel, out_shape=(jax.ShapeDtypeStruct((2, 128), F32),) *...  82.1 us
    unnamed x3, local copies, waits for them, and re-layouts  3.67 us

profile of v2, /device:TPU:1, one launch (start us, length us, event | category | flops | bytes accessed | tf_op | source)
XLA Modules:
  0.0 86.4 jit_solution(747537568964289733)
XLA Ops:
  0.6 82.1 %shard_map.76 = (f32[2,128]{1,0:T(2,128)}, f32[2,128]{1,0:T(2,128)}, f32[2,128]{1,0:T(2,128)}) custom-call(bf16[320,128]{1,0:T(8,128)(2,1)} %bitcast.3, bf16[2,320,128]{2,1,0:T(8,128)(2,1)} %bitcast.2, f32[320]{0:T(512)} %gain_hbm.1, bf16[1188,5120]{1,0:T(8,128)(2,1)} %unembed_hbm.1, s32[128]{0:T(128)} %targets_hbm.1), custom_call_target="tpu_custom_call" | custom-call | tf_op jit(solution)/shard_map/pallas_call | solution.py:650
  82.8 1.2 %copy.11 = f32[2,128]{1,0:T(2,128)} copy(f32[2,128]{1,0:T(2,128)} %get-tuple-element.6) | data formatting | bytes 2048
  84.0 1.2 %copy.12 = f32[2,128]{1,0:T(2,128)} copy(f32[2,128]{1,0:T(2,128)} %get-tuple-element.7) | data formatting | bytes 2048
  85.2 1.2 %copy.13 = f32[2,128]{1,0:T(2,128)} copy(f32[2,128]{1,0:T(2,128)} %get-tuple-element.8) | data formatting | bytes 2048

commit v3 on v2

v3 whole, which is shorter than its diff:
```python
import functools

import jax
import jax.numpy as jnp
from jax import lax
from jax.experimental import pallas as pl
from jax.experimental.pallas import tpu as pltpu
from jax.sharding import Mesh
from jax.sharding import PartitionSpec as P

MESH = pl.DeviceIdType.MESH
F32 = jnp.float32
BF16 = jnp.bfloat16
EPSILON = 1e-06

VOCAB = ("vocab_0", "vocab_1")
SECTION_VOCAB = ("section", "vocab_0", "vocab_1")

LINKS = ((0, 1), (0, -1), (1, 1), (1, -1), (2, 1), (2, -1))
TREE = (
    (-1, 0, 0, 1), (0, -1, 0, 3), (0, 0, -1, 5), (0, 0, 1, 4), (0, 1, 0, 2), (1, 0, 0, 0),
    (-1, -1, 0, 1), (-1, 0, -1, 1), (-1, 0, 1, 1), (-1, 1, 0, 1), (0, -1, -1, 5), (0, -1, 1, 4),
    (0, 0, 2, 4), (0, 1, -1, 5), (0, 1, 1, 2), (0, 2, 0, 2), (1, -1, 0, 3), (1, 0, -1, 0),
    (1, 0, 1, 0), (1, 1, 0, 2), (2, 0, 0, 0), (-1, -1, -1, 3), (-1, -1, 1, 1), (-1, 0, 2, 5),
    (-1, 1, -1, 5), (-1, 1, 1, 1), (-1, 2, 0, 2), (0, -1, 2, 4), (0, 1, 2, 2), (0, 2, -1, 3),
    (0, 2, 1, 3), (1, -1, -1, 0), (1, -1, 1, 4), (1, 0, 2, 4), (1, 1, -1, 2), (1, 1, 1, 2),
    (1, 2, 0, 3), (2, -1, 0, 0), (2, 0, -1, 0), (2, 0, 1, 0), (2, 1, 0, 0), (-1, -1, 2, 4),
    (-1, 1, 2, 5), (-1, 2, -1, 5), (-1, 2, 1, 3), (0, 2, 2, 5), (1, -1, 2, 5), (1, 1, 2, 4),
    (1, 2, -1, 0), (1, 2, 1, 3), (2, -1, -1, 0), (2, -1, 1, 3), (2, 0, 2, 5), (2, 1, -1, 1),
    (2, 1, 1, 1), (2, 2, 0, 3), (-1, 2, 2, 4), (1, 2, 2, 4), (2, -1, 2, 3), (2, 1, 2, 5),
    (2, 2, -1, 2), (2, 2, 1, 1), (2, 2, 2, 1),
)
PLAN = (
    (
        (1, 0, 0), (1, 1, 0), (1, 2, 0), (1, 3, 0), (1, 4, 0), (1, 5, 0), (1, 0, 1), (1, 1, 1), (1, 2, 1),
        (1, 3, 1), (1, 4, 1), (1, 5, 1), (1, 0, 2), (1, 1, 2), (1, 2, 2), (1, 3, 2), (1, 4, 2), (1, 5, 2),
        (1, 0, 3), (1, 1, 3), (1, 2, 3), (1, 3, 3), (1, 4, 3), (1, 5, 3), (0, 0, 0), (0, 1, 0), (0, 2, 0),
        (0, 3, 0), (0, 4, 0), (0, 5, 0), (1, 9, 0), (1, 10, 0), (1, 11, 0), (1, 14, 0), (1, 16, 0), (1, 17, 0),
        (1, 18, 0), (0, 0, 1), (0, 1, 1), (0, 2, 1), (0, 3, 1), (0, 4, 1), (0, 5, 1), (1, 9, 1), (1, 10, 1),
        (1, 11, 1), (1, 14, 1), (1, 16, 1), (1, 7, 0), (1, 17, 1), (0, 0, 2), (0, 1, 2), (0, 2, 2), (0, 3, 2),
        (0, 4, 2), (0, 5, 2), (1, 10, 2), (1, 11, 2), (1, 14, 2), (1, 16, 2), (1, 9, 2), (1, 18, 1), (0, 0, 3),
        (0, 1, 3), (0, 2, 3), (0, 3, 3), (0, 4, 3), (0, 5, 3), (1, 10, 3), (1, 11, 3), (1, 14, 3), (1, 16, 3),
        (1, 6, 0), (1, 12, 0), (1, 13, 0), (1, 15, 0), (1, 17, 2), (1, 12, 1), (1, 15, 1), (0, 9, 0), (0, 10, 0),
        (0, 11, 0), (0, 14, 0), (0, 16, 0), (0, 17, 0), (1, 22, 0), (1, 24, 0), (1, 29, 0), (1, 38, 0), (1, 13, 1),
        (1, 31, 0), (1, 32, 0), (0, 9, 1), (0, 10, 1), (0, 11, 1), (0, 14, 1), (0, 16, 1), (0, 18, 0), (1, 22, 1),
        (1, 29, 1), (1, 35, 0), (1, 25, 0), (1, 12, 2), (1, 13, 2), (1, 19, 0), (1, 39, 0), (0, 7, 0), (0, 10, 2),
        (0, 11, 2), (0, 14, 2), (0, 16, 2), (0, 17, 1), (1, 29, 2), (1, 22, 2), (1, 12, 3), (1, 13, 3), (1, 15, 2),
        (1, 37, 0), (0, 9, 2), (0, 10, 3), (0, 11, 3), (0, 14, 3), (0, 16, 3), (0, 18, 1), (1, 29, 3), (1, 30, 0),
        (1, 8, 0), (1, 27, 0), (0, 6, 0), (0, 12, 0), (0, 13, 0), (0, 15, 0), (0, 17, 2), (1, 28, 0), (0, 29, 0),
        (1, 45, 0), (1, 48, 0), (1, 27, 1), (1, 38, 1), (0, 22, 0), (0, 24, 0), (0, 12, 1), (0, 15, 1), (0, 38, 0),
        (1, 44, 0), (1, 28, 1), (1, 53, 0), (1, 30, 1), (0, 29, 1), (1, 45, 1), (1, 7, 1), (1, 27, 2), (1, 15, 3),
        (1, 31, 1), (0, 22, 1), (0, 13, 1), (0, 31, 0), (0, 32, 0), (0, 35, 0), (1, 49, 0), (0, 29, 2), (1, 45, 2),
        (1, 25, 1), (1, 27, 3), (1, 18, 2), (0, 25, 0), (0, 12, 2), (0, 13, 2), (0, 19, 0), (0, 39, 0), (1, 28, 2),
        (1, 30, 2), (0, 29, 3), (1, 45, 3), (1, 24, 1), (1, 32, 1), (1, 50, 0), (1, 54, 0), (0, 22, 2), (0, 12, 3),
        (0, 13, 3), (0, 15, 2), (0, 37, 0), (1, 28, 3), (1, 30, 3), (0, 30, 0), (1, 26, 0), (1, 20, 0), (1, 52, 0),
        (0, 8, 0), (0, 27, 0), (0, 28, 0), (0, 45, 0), (0, 48, 0),
    ),
    (
        (1, 44, 1), (0, 44, 0), (1, 56, 0), (1, 61, 0),
    ),
    (
        (1, 9, 3), (1, 46, 0), (1, 34, 0), (1, 47, 0), (1, 40, 0), (0, 27, 1), (0, 28, 1), (0, 45, 1), (0, 38, 1),
        (0, 53, 0), (1, 36, 0), (0, 30, 1),
    ),
    (
        (1, 22, 3), (1, 23, 0), (1, 17, 3), (1, 35, 1), (0, 7, 1), (0, 27, 2), (0, 15, 3), (0, 45, 2), (0, 31, 1),
        (1, 21, 0), (0, 49, 0), (1, 57, 0),
    ),
    (
        (1, 6, 1), (1, 42, 0), (1, 33, 0), (1, 19, 1), (1, 39, 1), (0, 25, 1), (0, 27, 3), (0, 28, 2), (0, 45, 3),
        (0, 18, 2), (0, 30, 2),
    ),
    (
        (1, 41, 0), (1, 26, 1), (1, 37, 1), (1, 59, 0), (0, 24, 1), (0, 28, 3), (0, 32, 1), (0, 50, 0), (0, 54, 0),
        (1, 49, 1), (1, 53, 1), (1, 51, 0), (0, 30, 3),
    ),
    (
        (1, 48, 1), (1, 60, 0), (0, 26, 0), (0, 56, 0), (0, 20, 0), (0, 52, 0), (0, 61, 0), (1, 43, 0), (1, 62, 0),
        (1, 58, 0), (0, 44, 1), (1, 56, 1),
    ),
    (
        (1, 8, 1), (1, 24, 2), (1, 32, 2), (1, 34, 1), (1, 38, 2), (0, 9, 3), (0, 46, 0), (0, 34, 0), (0, 47, 0),
        (0, 40, 0), (1, 55, 0), (0, 36, 0),
    ),
    (
        (1, 7, 2), (1, 31, 2), (1, 35, 2), (1, 52, 1), (0, 22, 3), (0, 23, 0), (0, 17, 3), (0, 35, 1), (0, 57, 0),
        (1, 47, 1), (1, 44, 2), (0, 21, 0), (1, 25, 2), (1, 46, 1), (1, 18, 3), (1, 19, 2), (0, 6, 1), (0, 42, 0),
        (0, 33, 0), (0, 19, 1), (0, 39, 1),
    ),
    (
        (1, 36, 1), (0, 49, 1), (1, 57, 1), (1, 23, 1), (1, 26, 2), (1, 33, 1), (1, 50, 1), (1, 54, 1), (0, 41, 0),
        (0, 26, 1), (0, 37, 1), (0, 53, 1), (0, 59, 0),
    ),
    (
        (1, 21, 1), (0, 51, 0), (1, 41, 1), (1, 42, 1), (1, 20, 1), (1, 60, 1), (0, 43, 0), (0, 56, 1), (0, 48, 1),
        (0, 60, 0), (0, 62, 0), (1, 62, 1),
    ),
    (
        (0, 58, 0), (1, 43, 1), (1, 32, 3), (1, 34, 2), (1, 40, 1), (1, 61, 1), (0, 8, 1), (0, 24, 2), (0, 32, 2),
        (0, 34, 1), (0, 38, 2), (1, 49, 2),
    ),
    (
        (1, 51, 1), (0, 55, 0), (1, 19, 3), (1, 39, 2), (1, 53, 2), (1, 59, 1), (0, 7, 2), (0, 31, 2), (0, 35, 2),
        (0, 47, 1), (0, 52, 1), (1, 58, 1),
    ),
    (
        (0, 44, 2), (1, 56, 2), (1, 6, 2), (1, 24, 3), (1, 47, 2), (1, 37, 2), (0, 25, 2), (0, 46, 1), (0, 18, 3),
        (0, 19, 2), (0, 57, 1), (1, 35, 3), (1, 55, 1),
    ),
    (
        (0, 36, 1), (1, 8, 2), (1, 26, 3), (1, 33, 2), (1, 48, 2), (1, 52, 2), (0, 23, 1), (0, 26, 2), (0, 33, 1),
        (0, 50, 1), (0, 54, 1), (1, 44, 3),
    ),
    (
        (0, 21, 1), (1, 7, 3), (1, 46, 2), (1, 34, 3), (1, 38, 3), (0, 41, 1), (0, 42, 1), (0, 20, 1), (0, 60, 1),
        (0, 62, 1), (1, 36, 2), (0, 49, 2), (1, 57, 2),
    ),
    (
        (1, 41, 2), (1, 23, 2), (1, 25, 3), (1, 31, 3), (0, 43, 1), (0, 32, 3), (0, 34, 2), (0, 40, 1), (0, 61, 1),
        (1, 49, 3), (0, 51, 1),
    ),
    (
        (1, 42, 2), (1, 33, 3), (1, 50, 2), (0, 56, 2), (0, 19, 3), (0, 39, 2), (0, 53, 2), (0, 59, 1), (1, 60, 2),
        (1, 62, 2), (1, 21, 2), (0, 58, 1),
    ),
    (
        (1, 43, 2), (1, 20, 2), (1, 54, 2), (0, 6, 2), (0, 24, 3), (0, 35, 3), (0, 47, 2), (0, 37, 2), (1, 47, 3),
        (1, 51, 2), (0, 55, 1), (1, 40, 2), (1, 59, 2), (1, 61, 2),
    ),
    (
        (0, 8, 2), (0, 26, 3), (0, 33, 2), (0, 48, 2), (0, 52, 2), (1, 58, 2), (0, 44, 3), (1, 56, 3), (1, 41, 3),
        (1, 39, 3), (1, 53, 3),
    ),
    (
        (0, 7, 3), (0, 46, 2), (0, 34, 3), (0, 57, 2), (0, 38, 3), (1, 52, 3), (1, 55, 2), (0, 36, 2), (1, 6, 3),
        (1, 37, 3),
    ),
    (
        (0, 41, 2), (0, 23, 2), (0, 25, 3), (0, 31, 3), (1, 46, 3), (1, 36, 3), (0, 49, 3), (0, 60, 2), (1, 57, 3),
        (1, 8, 3), (1, 23, 3), (1, 48, 3), (0, 42, 2), (0, 33, 3), (0, 50, 2), (0, 62, 2),
    ),
    (
        (1, 21, 3), (0, 21, 2), (1, 42, 3), (1, 50, 3), (1, 54, 3), (0, 43, 2), (0, 47, 3), (0, 20, 2), (0, 54, 2),
    ),
    (
        (0, 51, 2), (1, 43, 3), (1, 20, 3), (0, 56, 3), (0, 40, 2), (0, 59, 2), (0, 61, 2), (1, 62, 3),
    ),
    (
        (0, 58, 2), (1, 40, 3), (1, 61, 3), (0, 41, 3), (0, 39, 3), (0, 52, 3), (0, 53, 3), (1, 51, 3), (1, 59, 3),
        (1, 60, 3), (1, 58, 3), (0, 55, 2),
    ),
    (
        (0, 6, 3), (0, 46, 3), (0, 57, 3), (0, 37, 3), (1, 55, 3), (0, 36, 3),
    ),
    (
        (0, 8, 3), (0, 23, 3), (0, 48, 3), (0, 21, 3),
    ),
    (
        (0, 42, 3), (0, 50, 3), (0, 54, 3),
    ),
    (
        (0, 43, 3), (0, 20, 3), (0, 62, 3), (0, 51, 3), (0, 60, 3),
    ),
    (
        (0, 40, 3), (0, 59, 3), (0, 61, 3), (0, 58, 3),
    ),
    (
        (0, 55, 3),
    ),
    (),
    (),
    (),
    (),
)
PLANES = (0, 1, -1, 2)

GROUPS = 4
GTOK = 16
FILL = -1e30


def dispatch(index, branches, low=0, high=None):
    high = len(branches) if high is None else high
    if not any(branches[low:high]):
        return
    if high - low == 1:
        branches[low]()
        return
    mid = (low + high) // 2

    @pl.when(index < mid)
    def _():
        dispatch(index, branches, low, mid)

    @pl.when(index >= mid)
    def _():
        dispatch(index, branches, mid, high)


def kernel(
    stream_hbm, deltas_hbm, gain_hbm, unembed_hbm, targets_hbm, out_ref,
    stream_v, deltas_v, targets_v, gain_v, gains, outbox, gat, words, rows_a, rows_b, rows_c, acc, final,
    squares, scales, tops, sums, stats, slices, from_section, partial, from_plane,
    load_sem, own_sem, words_send, words_recv, gain_send, gain_recv,
    part_send, part_recv, send_sem, recv_sem,
    section_send, section_recv, plane_send, plane_recv,
):
    section = lax.axis_index("section")
    x = lax.axis_index("vocab_0")
    z = lax.axis_index("vocab_1")
    y = section // 2
    core = section % 2
    sign = 1 - 2 * core
    nwords = unembed_hbm.shape[0]
    plane_width = unembed_hbm.shape[1] // 4
    home = (x, y, z)

    def device(xx, yy, zz, cc):
        return (yy * 2 + cc, xx, zz)

    def moved(axis, step):
        at = list(home)
        at[axis] = lax.rem(at[axis] + step + 4, 4)
        return tuple(at)

    neighbours = [device(*moved(axis, way * sign), core) for axis, way in LINKS]
    partner = device(x, y, z, 1 - core)
    source = [{d: lax.rem(home[axis] - sign * d + 4, 4) for d in (-1, 0, 1, 2)} for axis in range(3)]

    loads = [
        pltpu.make_async_copy(stream_hbm, stream_v, load_sem.at[0]),
        pltpu.make_async_copy(deltas_hbm, deltas_v, load_sem.at[1]),
        pltpu.make_async_copy(targets_hbm, targets_v, load_sem.at[2]),
        pltpu.make_async_copy(gain_hbm, gain_v, load_sem.at[3]),
    ]
    for copy in loads:
        copy.start()

    def plane_peer(step):
        return device(lax.rem(x + step // 4, 4), y, lax.rem(z + step % 4, 4), core)

    def section_peer(step, other):
        return device(x, lax.rem(y + step, 4), z, 1 - core if other else core)

    section_peers = [(step, other) for step in range(4) for other in (0, 1) if step or other]
    barrier = pltpu.get_barrier_semaphore()
    around = [device(*moved(axis, way), cc) for axis, way in LINKS for cc in range(2)]
    for peer in around + [partner]:
        pl.semaphore_signal(barrier, inc=1, device_id=peer, device_id_type=MESH)

    def columns(plane):
        return pl.ds(pl.multiple_of(plane * plane_width, 128), plane_width)

    own_words = []
    for p, dx in enumerate(PLANES):
        plane = source[0][dx]
        own_words.append(
            pltpu.make_async_copy(
                unembed_hbm.at[:, columns(plane)], words.at[0, plane, pl.ds(0, nwords)], own_sem.at[p]
            )
        )
        own_words[-1].start()

    for copy in loads:
        copy.wait()

    lane = lax.broadcasted_iota(jnp.int32, (GTOK, 128), 1)
    low = lane < 64
    odd = lax.rem(z, 2) == 1
    my_slot = ((x * 4 + y) * 4 + z) * GROUPS

    first = jnp.where(section == 0, 1.0, 0.0).astype(F32)
    former = deltas_v[0].astype(F32) + stream_v[...].astype(F32) * first
    kept = former.astype(BF16).astype(F32)
    latter = deltas_v[1].astype(F32) + (former - kept)
    packed = []
    heads = []
    for value in (kept, latter):
        packed.append(jnp.where(odd, value[64:192], value[0:128]))
        packed.append(jnp.where(odd, value[192:320], value[128:256]))
        heads.append(jnp.where(odd, value[0:64], value[256:320]))
    lead = jnp.where(odd, heads[1], heads[0])
    trail = jnp.where(odd, heads[0], heads[1])
    packed.append(jnp.concatenate([lead, trail], axis=0))
    for k, value in enumerate(packed):
        tile = jnp.transpose(value).astype(BF16)
        for half in range(2):

            @pl.when(core == half)
            def _():
                for g in range(GROUPS):
                    t0 = half * 64 + g * GTOK
                    gat[my_slot + g, core, k] = tile[t0 : t0 + GTOK]

            @pl.when(core != half)
            def _():
                for g in range(GROUPS):
                    t0 = half * 64 + g * GTOK
                    outbox[g, k] = tile[t0 : t0 + GTOK]

    low_row = lax.broadcasted_iota(jnp.int32, (1, 128), 1) < 64
    none = jnp.zeros((1, 64), F32)
    g0 = gain_v[0:128].reshape(1, 128)
    g1 = gain_v[128:256].reshape(1, 128)
    g2 = jnp.concatenate([gain_v[256:320].reshape(1, 64), none], axis=1)
    t0, t1, t2 = (pltpu.roll(v, 64, 1) for v in (g0, g1, g2))
    blank = jnp.zeros((1, 128), F32)
    gain_rows = (
        (g0, blank),
        (g1, blank),
        (g2, jnp.where(low_row, 0.0, t0)),
        (blank, jnp.where(low_row, t0, t1)),
        (blank, jnp.where(low_row, t1, t2)),
    )
    gains[x * 4 + z] = jnp.concatenate(
        [jnp.where(odd, other, even) for even, other in gain_rows] + [blank] * 3, axis=0
    )

    final[:, 1184:1200, :] = jnp.full((2, 16, 256), FILL, F32)

    pl.semaphore_wait(barrier, 13)

    part = pltpu.make_async_remote_copy(
        src_ref=outbox,
        dst_ref=gat.at[pl.ds(my_slot, GROUPS), core],
        send_sem=part_send,
        recv_sem=part_recv,
        device_id=partner,
        device_id_type=MESH,
    )
    part.start()

    def gain_copy(n, link):
        at = (source[0][n[0]] * 4 + source[2][n[2]])
        place = (TREE_INDEX[child(n, link)] if link is not None else TREE_INDEX[n])
        return pltpu.make_async_remote_copy(
            src_ref=gains.at[at],
            dst_ref=gains.at[at],
            send_sem=gain_send.at[GAIN_INDEX[place]],
            recv_sem=gain_recv.at[GAIN_INDEX[place]],
            device_id=neighbours[link or 0],
            device_id_type=MESH,
        )

    def block_copy(n, row, link, g):
        slot = source[0][n[0]] * 64 + source[1][n[1]] * 16 + source[2][n[2]] * 4 + g
        return pltpu.make_async_remote_copy(
            src_ref=gat.at[slot],
            dst_ref=gat.at[slot],
            send_sem=send_sem.at[g],
            recv_sem=recv_sem.at[row * GROUPS + g],
            device_id=neighbours[link],
            device_id_type=MESH,
        )

    def first_copy(row, link, g, away):
        axis, way = LINKS[link]
        return pltpu.make_async_remote_copy(
            src_ref=outbox.at[g] if away else gat.at[my_slot + g, core],
            dst_ref=gat.at[my_slot + g, core],
            send_sem=send_sem.at[g],
            recv_sem=recv_sem.at[row * GROUPS + g],
            device_id=device(*moved(axis, -way * sign), 1 - core) if away else neighbours[link],
            device_id_type=MESH,
        )

    def send_gain(n):
        for row, (dx, dy, dz, link) in enumerate(TREE):
            if dy == 0 and parent((dx, dy, dz), link) == n:
                gain_copy(n, link).start()

    def run(actions):
        for kind, row, g in actions:
            dx, dy, dz, link = TREE[row]
            n = (dx, dy, dz)
            if kind == 0:
                block_copy(n, row, link, g).wait_recv()
                if g == 0 and dy == 0:
                    gain_copy(n, None).wait_recv()
                    send_gain(n)
            elif parent(n, link) == (0, 0, 0):
                for away in (False, True):
                    first_copy(row, link, g, away).start()
            else:
                block_copy(parent(n, link), row, link, g).start()

    send_gain((0, 0, 0))

    their_words = []
    for p, dx in enumerate(PLANES):
        plane = lax.rem(x + sign * dx + 4, 4)
        their_words.append(
            pltpu.make_async_remote_copy(
                src_ref=unembed_hbm.at[:, columns(plane)],
                dst_ref=words.at[1, plane, pl.ds(0, nwords)],
                send_sem=words_send.at[p],
                recv_sem=words_recv.at[p],
                device_id=partner,
                device_id_type=MESH,
            )
        )

    for copy in their_words:
        copy.start()

    segment = lax.broadcasted_iota(jnp.int32, (1, 128), 1) // GTOK

    def spread(value):
        for step in (16, 32, 64):
            value = value + pltpu.roll(value, step, 1)
        return value

    def prepare(g, p, zp, rows):
        plane = source[0][PLANES[p]]
        running = [jnp.zeros((GTOK, 128), F32) for _ in range(5)]
        both = gains[plane * 4 + 2 * zp] + gains[plane * 4 + 2 * zp + 1]
        factor = [jnp.broadcast_to(both[k : k + 1, :], (GTOK, 128)) for k in range(5)]
        for yy in range(4):
            even = plane * 64 + yy * 16 + 2 * zp * 4 + g
            other = even + 4
            for cc in range(2):
                pe = gat[even, cc, 4].astype(F32)
                po = gat[other, cc, 4].astype(F32)
                for l in range(2):
                    layer = 4 * yy + 2 * cc + l
                    if l == 0:
                        middle = jnp.where(low, pe, po)
                    else:
                        middle = pltpu.roll(jnp.where(low, po, pe), 64, 1)
                    values = [
                        gat[even, cc, 2 * l].astype(F32),
                        gat[even, cc, 2 * l + 1].astype(F32),
                        middle,
                        gat[other, cc, 2 * l].astype(F32),
                        gat[other, cc, 2 * l + 1].astype(F32),
                    ]
                    span = slice(layer * GTOK, (layer + 1) * GTOK)
                    total = jnp.zeros((GTOK, 128), F32) if p == 0 and zp == 0 else squares[g, span, :]
                    for k in range(5):
                        at = 5 * zp + k
                        running[k] = running[k] + values[k]
                        total = total + running[k] * running[k]
                        rows[span, at * 128 : (at + 1) * 128] = (running[k] * factor[k]).astype(BF16)
                    squares[g, span, :] = total

    def multiply(g, p, stretch, rows):
        start, stop = ((0, 592), (592, nwords))[stretch]
        plane = source[0][PLANES[p]]
        most = []
        for half in range(2):
            product = lax.dot_general(
                words[half, plane, start:stop, :], rows[...], (((1,), (1,)), ((), ())), preferred_element_type=F32
            )
            if p == 0:
                acc[g, half, start:stop, :] = product
            elif p < 3:
                acc[g, half, start:stop, :] = acc[g, half, start:stop, :] + product
            else:
                total = acc[g, half, start:stop, :] + product
                final[half, start:stop, :] = total
                most.append(jnp.max(total[0:592].reshape(74, 8, 256), axis=0))
                if stop - start > 592:
                    most.append(jnp.broadcast_to(jnp.max(total[592:], axis=0, keepdims=True), (8, 256)))
        if p == 3:
            if stretch == 1:
                most.append(tops[...])
            tops[...] = functools.reduce(jnp.maximum, most)

    def scaled(g):
        total = jnp.sum(jnp.transpose(squares[g]), axis=0, keepdims=True)
        scales[0:1, :] = lax.rsqrt(total / (4 * plane_width) + EPSILON)

    def peaked():
        scales[1:2, :] = jnp.max(tops[...], axis=0, keepdims=True) * scales[0:1, :]

    def folded(g, half):
        scale = jnp.broadcast_to(scales[0:1, :], (8, 256))
        peaks = jnp.broadcast_to(scales[1:2, :], (8, 256))
        sublane = lax.broadcasted_iota(jnp.int32, (8, 256), 0)
        holder = core if half == 0 else 1 - core
        first_word = (((y * 2 + holder) * 4 + x) * 4 + z) * nwords
        local = targets_v[...].reshape(1, 128) - first_word
        local = jnp.where(local < nwords, local, -8)
        local = spread(jnp.where(segment == core * GROUPS + g, local, 0))
        wanted = jnp.broadcast_to(jnp.concatenate([local, local], axis=1), (8, 256)) - sublane
        if half == 0:
            mass = moment = picked = jnp.zeros((8, 256), F32)
        else:
            mass, moment, picked = (sums[k] for k in range(3))
        for k in range(150):
            z_all = final[half, 8 * k : 8 * k + 8, :] * scale
            z_rel = z_all - peaks
            e = jnp.exp(z_rel)
            mass = mass + e
            moment = moment + e * z_rel
            picked = jnp.where(wanted == 8 * k, z_all, picked)
        if half == 0:
            for k, value in enumerate((mass, moment, picked)):
                sums[k] = value
            return
        found = [scales[1:2, :]] + [jnp.sum(v, axis=0, keepdims=True) for v in (mass, moment, picked)]
        for k, value in enumerate(found):
            stats[g, 2 * k : 2 * k + 1, :] = value[:, 0:128]
            stats[g, 2 * k + 1 : 2 * k + 2, :] = value[:, 128:256]

    def words_ready(p):
        plane = source[0][PLANES[p]]
        own_words[p].wait()
        pltpu.make_async_remote_copy(
            src_ref=unembed_hbm.at[:, columns(plane)],
            dst_ref=words.at[1, plane, pl.ds(0, nwords)],
            send_sem=words_send.at[p],
            recv_sem=words_recv.at[p],
            device_id=partner,
            device_id_type=MESH,
        ).wait_recv()

    run(PLAN[0])
    part.wait_recv()
    for zp in range(2):
        prepare(0, 0, zp, rows_c)
    run(PLAN[1])
    words_ready(0)
    multiply(0, 0, 0, rows_c)
    run(PLAN[2])
    multiply(0, 0, 1, rows_c)
    run(PLAN[3])
    for zp in range(2):
        prepare(1, 0, zp, rows_a)
    for g, now, later in ((1, rows_a, rows_b), (2, rows_b, rows_c), (3, rows_c, rows_a)):
        for k in range(2):
            run(PLAN[2 + 2 * g + k])
            multiply(g, 0, k, now)
            prepare(*((g + 1, 0) if g < 3 else (0, 1)), k, later)

    def body(g, carry):
        rotation = (rows_a, rows_b, rows_c)
        for p in (1, 2, 3):
            now, later = rotation[p - 1], rotation[p % 3]
            following = (g, p + 1) if p < 3 else (jnp.minimum(g + 1, GROUPS - 1), 1)
            former_group = lax.rem(g + GROUPS - 1, GROUPS)
            if p == 3:
                scaled(g)
            for k in range(2):
                rows_of_plan = [PLAN[10 + 6 * j + 2 * (p - 1) + k] for j in range(GROUPS)]
                dispatch(g, [functools.partial(run, row) if row else None for row in rows_of_plan])
                if k == 0:
                    pl.when(g == 0)(functools.partial(words_ready, p))
                multiply(g, p, k, now)
                prepare(*following, k, later)
                if p == 1:
                    folded(former_group, k)
            if p == 3:
                peaked()
        return carry

    lax.fori_loop(0, GROUPS, body, 0)
    run(PLAN[34])
    for half in range(2):
        folded(GROUPS - 1, half)

    def joined(parts):
        most = functools.reduce(jnp.maximum, [part[0] for part in parts])
        shifts = [part[0] - most for part in parts]
        factors = [jnp.exp(shift) for shift in shifts]
        mass = sum(f * part[1] for f, part in zip(factors, parts))
        moment = sum(f * (part[2] + shift * part[1]) for f, shift, part in zip(factors, shifts, parts))
        return most, mass, moment, sum(part[3] for part in parts)

    wide_segment = lax.broadcasted_iota(jnp.int32, (8, 128), 1) // 32
    for q in range(4):
        value = jnp.zeros((8, 128), F32)
        for g in range(GROUPS):
            shift = 32 * ((g - q) % 4)
            moved_row = pltpu.roll(stats[g], shift, 1) if shift else stats[g]
            value = jnp.where(wide_segment == g, moved_row, value)
        for half in range(2):
            for k in range(4):
                slices[half * 4 + q, k : k + 1, :] = value[2 * k + half : 2 * k + half + 1, :]

    def section_copy(step, other):
        yy = lax.rem(y + step, 4)
        cc = 1 - core if other else core
        at = step * 2 + other
        return pltpu.make_async_remote_copy(
            src_ref=slices.at[yy * 2 + cc],
            dst_ref=from_section.at[at],
            send_sem=section_send.at[at],
            recv_sem=section_recv.at[at],
            device_id=section_peer(step, other),
            device_id_type=MESH,
        )

    for p in section_peers:
        section_copy(*p).start()
    from_section[0] = slices[section]
    for p in section_peers:
        section_copy(*p).wait_recv()
    for other in range(2):
        arrived = [from_section[2 * step + other] for step in range(4)]
        found = joined([[part[k : k + 1] for k in range(4)] for part in arrived])
        for k, value in enumerate(found):
            row = 4 * (core if other == 0 else 1 - core) + k
            partial[pl.ds(row, 1), :] = value

    def plane_copy(step):
        return pltpu.make_async_remote_copy(
            src_ref=partial,
            dst_ref=from_plane.at[step],
            send_sem=plane_send.at[step],
            recv_sem=plane_recv.at[step],
            device_id=plane_peer(step),
            device_id_type=MESH,
        )

    for step in range(1, 16):
        plane_copy(step).start()
    from_plane[0] = partial[...]
    for step in range(1, 16):
        plane_copy(step).wait_recv()
    everything = [from_plane[step] for step in range(16)]
    narrow = lax.broadcasted_iota(jnp.int32, (1, 128), 1)
    result = [[jnp.zeros((1, 128), F32) for _ in range(2)] for _ in range(3)]
    for half in range(2):
        most, mass, moment, picked = joined([[part[4 * half + k : 4 * half + k + 1] for k in range(4)] for part in everything])
        log_mass = jnp.log(mass)
        lse = most + log_mass
        for n, value in enumerate((lse, log_mass - moment / mass, picked - lse)):
            for l in range(2):
                for g in range(GROUPS):
                    shift = (64 * half + 16 * g - 32 * g - 16 * l) % 128
                    moved_row = pltpu.roll(value, shift, 1) if shift else value
                    result[n][l] = jnp.where(narrow // GTOK == 4 * half + g, moved_row, result[n][l])
    for n in range(3):
        for l in range(2):
            out_ref[n, l : l + 1, :] = result[n][l]

    for p in section_peers:
        section_copy(*p).wait_send()
    for step in range(1, 16):
        plane_copy(step).wait_send()
    part.wait_send()
    for copy in their_words:
        copy.wait_send()
    for row, (dx, dy, dz, link) in enumerate(TREE):
        if dy == 0:
            gain_copy(parent((dx, dy, dz), link), link).wait_send()
    for g in range(GROUPS):
        pltpu.make_async_remote_copy(
            src_ref=gat.at[pl.ds(0, len(TREE))],
            dst_ref=gat.at[pl.ds(0, len(TREE))],
            send_sem=send_sem.at[g],
            recv_sem=recv_sem.at[0],
            device_id=neighbours[0],
            device_id_type=MESH,
        ).wait_send()


def wrapped(c):
    return (c + 1) % 4 - 1


def parent(n, link):
    axis, way = LINKS[link]
    n = list(n)
    n[axis] = wrapped(n[axis] - way)
    return tuple(n)


def child(n, link):
    axis, way = LINKS[link]
    n = list(n)
    n[axis] = wrapped(n[axis] + way)
    return tuple(n)


TREE_INDEX = {row[:3]: k for k, row in enumerate(TREE)}
GAIN_INDEX = {k: i for i, k in enumerate(k for k, row in enumerate(TREE) if row[1] == 0)}


def shards(stream_in, deltas, norm_gain, unembed, targets):
    nwords, width = unembed.shape
    anywhere = pl.BlockSpec(memory_space=pl.ANY)
    inside = pl.BlockSpec(memory_space=pltpu.VMEM)
    dma = pltpu.SemaphoreType.DMA
    out = pl.pallas_call(
        kernel,
        out_shape=jax.ShapeDtypeStruct((3, 2, 128), F32),
        in_specs=[anywhere] * 5,
        out_specs=inside,
        scratch_shapes=[
            pltpu.VMEM((320, 128), BF16),
            pltpu.VMEM((2, 320, 128), BF16),
            pltpu.VMEM((128,), jnp.int32),
            pltpu.VMEM((320,), F32),
            pltpu.VMEM((16, 8, 128), F32),
            pltpu.VMEM((GROUPS, 5, GTOK, 128), BF16),
            pltpu.VMEM((64 * GROUPS, 2, 5, GTOK, 128), BF16),
            pltpu.VMEM((2, 4, nwords, width // 4), BF16),
            pltpu.VMEM((256, width // 4), BF16),
            pltpu.VMEM((256, width // 4), BF16),
            pltpu.VMEM((256, width // 4), BF16),
            pltpu.VMEM((GROUPS, 2, 1200, 256), F32),
            pltpu.VMEM((2, 1200, 256), F32),
            pltpu.VMEM((GROUPS, 256, 128), F32),
            pltpu.VMEM((8, 256), F32),
            pltpu.VMEM((8, 256), F32),
            pltpu.VMEM((3, 8, 256), F32),
            pltpu.VMEM((GROUPS, 8, 128), F32),
            pltpu.VMEM((8, 4, 128), F32),
            pltpu.VMEM((8, 4, 128), F32),
            pltpu.VMEM((8, 128), F32),
            pltpu.VMEM((16, 8, 128), F32),
            dma((4,)),
            dma((4,)),
            dma((4,)),
            dma((4,)),
            dma((15,)),
            dma((15,)),
            dma,
            dma,
            dma((GROUPS,)),
            dma((63 * GROUPS,)),
            dma((8,)),
            dma((8,)),
            dma((16,)),
            dma((16,)),
        ],
        compiler_params=pltpu.CompilerParams(
            collective_id=0, has_side_effects=True, vmem_limit_bytes=60 * 1024 * 1024
        ),
    )(stream_in.T, deltas.transpose(0, 2, 1), norm_gain, unembed, targets)
    return out[0], out[1], out[2]


def solution(mesh):
    torus = Mesh(
        mesh.devices.reshape(mesh.shape["section"], 4, 4), ("section", "vocab_0", "vocab_1")
    )
    placed = (P(None, VOCAB), P("section", None, VOCAB), P(VOCAB), P(SECTION_VOCAB, None), P())
    return jax.shard_map(
        shards,
        mesh=torus,
        in_specs=placed,
        out_specs=(P("section", None), P("section", None), P("section", None)),
        check_vma=False,
    )
```

time: 86.6 us -> 76.9 us (0.89)
  Pallas kernels: 82.1 us -> 74.9 us
  local copies, waits for them, and re-layouts: 3.67 us -> 1.25 us
    pallas_call x1, Pallas kernels: 82.1 us -> 74.9 us  [shards(): pl.pallas_call(kernel, out_shape=jax.ShapeDtypeStruct((3, 2, 128), F32),...]
    unnamed x3 -> x0, local copies, waits for them, and re-layouts: 3.67 us -> none
    squeeze x0 -> x1, local copies, waits for them, and re-layouts: none -> 1.25 us  [shards(): return (out[0], out[1], out[2])]
where the time goes in v3:
time: 76.9 us; the launch traced here: 76.8 us
  Pallas kernels  74.9 us (97%)
  local copies, waits for them, and re-layouts  1.25 us (2%)
    pallas_call x1, Pallas kernels, shards(): pl.pallas_call(kernel, out_shape=jax.ShapeDtypeStruct((3, 2, 128), F32),...  74.9 us

profile of v3, /device:TPU:1, one launch (start us, length us, event | category | flops | bytes accessed | tf_op | source)
XLA Modules:
  0.0 76.8 jit_solution(792357084405130722)
XLA Ops:
  0.6 74.9 %shard_map.76 = f32[3,2,128]{2,1,0:T(2,128)} custom-call(bf16[320,128]{1,0:T(8,128)(2,1)} %bitcast.9, bf16[2,320,128]{2,1,0:T(8,128)(2,1)} %bitcast.8, f32[320]{0:T(512)} %gain_hbm.1, bf16[1188,5120]{1,0:T(8,128)(2,1)} %unembed_hbm.1, s32[128]{0:T(128)} %targets_hbm.1), custom_call_target="tpu_custom_call" | custom-call | tf_op jit(solution)/shard_map/pallas_call | solution.py:686
  75.6 1.2 %slice_bitcast_fusion = (f32[2,128]{1,0:T(2,128)}, f32[2,128]{1,0:T(2,128)}, f32[2,128]{1,0:T(2,128)}) fusion(f32[3,2,128]{2,1,0:T(2,128)} %shard_map.76), kind=kLoop, calls=%fused_computation | loop fusion | bytes 6144 | tf_op jit(solution)/shard_map/squeeze | solution.py:733

commit v4 on v3

--- a/solution.py
+++ b/solution.py
@@ -19,15 +19,15 @@
 LINKS = ((0, 1), (0, -1), (1, 1), (1, -1), (2, 1), (2, -1))
 TREE = (
     (-1, 0, 0, 1), (0, -1, 0, 3), (0, 0, -1, 5), (0, 0, 1, 4), (0, 1, 0, 2), (1, 0, 0, 0),
-    (-1, -1, 0, 1), (-1, 0, -1, 1), (-1, 0, 1, 1), (-1, 1, 0, 1), (0, -1, -1, 5), (0, -1, 1, 4),
-    (0, 0, 2, 4), (0, 1, -1, 5), (0, 1, 1, 2), (0, 2, 0, 2), (1, -1, 0, 3), (1, 0, -1, 0),
-    (1, 0, 1, 0), (1, 1, 0, 2), (2, 0, 0, 0), (-1, -1, -1, 3), (-1, -1, 1, 1), (-1, 0, 2, 5),
-    (-1, 1, -1, 5), (-1, 1, 1, 1), (-1, 2, 0, 2), (0, -1, 2, 4), (0, 1, 2, 2), (0, 2, -1, 3),
-    (0, 2, 1, 3), (1, -1, -1, 0), (1, -1, 1, 4), (1, 0, 2, 4), (1, 1, -1, 2), (1, 1, 1, 2),
-    (1, 2, 0, 3), (2, -1, 0, 0), (2, 0, -1, 0), (2, 0, 1, 0), (2, 1, 0, 0), (-1, -1, 2, 4),
+    (-1, -1, 0, 3), (-1, 0, -1, 1), (-1, 0, 1, 1), (-1, 1, 0, 1), (0, -1, -1, 5), (0, -1, 1, 4),
+    (0, 0, 2, 4), (0, 1, -1, 5), (0, 1, 1, 2), (0, 2, 0, 2), (1, -1, 0, 0), (1, 0, -1, 0),
+    (1, 0, 1, 0), (1, 1, 0, 0), (2, 0, 0, 0), (-1, -1, -1, 3), (-1, -1, 1, 1), (-1, 0, 2, 5),
+    (-1, 1, -1, 5), (-1, 1, 1, 2), (-1, 2, 0, 1), (0, -1, 2, 3), (0, 1, 2, 4), (0, 2, -1, 3),
+    (0, 2, 1, 2), (1, -1, -1, 0), (1, -1, 1, 4), (1, 0, 2, 4), (1, 1, -1, 2), (1, 1, 1, 2),
+    (1, 2, 0, 3), (2, -1, 0, 0), (2, 0, -1, 0), (2, 0, 1, 1), (2, 1, 0, 2), (-1, -1, 2, 4),
     (-1, 1, 2, 5), (-1, 2, -1, 5), (-1, 2, 1, 3), (0, 2, 2, 5), (1, -1, 2, 5), (1, 1, 2, 4),
-    (1, 2, -1, 0), (1, 2, 1, 3), (2, -1, -1, 0), (2, -1, 1, 3), (2, 0, 2, 5), (2, 1, -1, 1),
-    (2, 1, 1, 1), (2, 2, 0, 3), (-1, 2, 2, 4), (1, 2, 2, 4), (2, -1, 2, 3), (2, 1, 2, 5),
+    (1, 2, -1, 3), (1, 2, 1, 3), (2, -1, -1, 0), (2, -1, 1, 1), (2, 0, 2, 5), (2, 1, -1, 2),
+    (2, 1, 1, 2), (2, 2, 0, 3), (-1, 2, 2, 4), (1, 2, 2, 4), (2, -1, 2, 3), (2, 1, 2, 5),
     (2, 2, -1, 2), (2, 2, 1, 1), (2, 2, 2, 1),
 )
 PLAN = (
@@ -35,138 +35,136 @@
         (1, 0, 0), (1, 1, 0), (1, 2, 0), (1, 3, 0), (1, 4, 0), (1, 5, 0), (1, 0, 1), (1, 1, 1), (1, 2, 1),
         (1, 3, 1), (1, 4, 1), (1, 5, 1), (1, 0, 2), (1, 1, 2), (1, 2, 2), (1, 3, 2), (1, 4, 2), (1, 5, 2),
         (1, 0, 3), (1, 1, 3), (1, 2, 3), (1, 3, 3), (1, 4, 3), (1, 5, 3), (0, 0, 0), (0, 1, 0), (0, 2, 0),
-        (0, 3, 0), (0, 4, 0), (0, 5, 0), (1, 9, 0), (1, 10, 0), (1, 11, 0), (1, 14, 0), (1, 16, 0), (1, 17, 0),
-        (1, 18, 0), (0, 0, 1), (0, 1, 1), (0, 2, 1), (0, 3, 1), (0, 4, 1), (0, 5, 1), (1, 9, 1), (1, 10, 1),
-        (1, 11, 1), (1, 14, 1), (1, 16, 1), (1, 7, 0), (1, 17, 1), (0, 0, 2), (0, 1, 2), (0, 2, 2), (0, 3, 2),
-        (0, 4, 2), (0, 5, 2), (1, 10, 2), (1, 11, 2), (1, 14, 2), (1, 16, 2), (1, 9, 2), (1, 18, 1), (0, 0, 3),
-        (0, 1, 3), (0, 2, 3), (0, 3, 3), (0, 4, 3), (0, 5, 3), (1, 10, 3), (1, 11, 3), (1, 14, 3), (1, 16, 3),
-        (1, 6, 0), (1, 12, 0), (1, 13, 0), (1, 15, 0), (1, 17, 2), (1, 12, 1), (1, 15, 1), (0, 9, 0), (0, 10, 0),
-        (0, 11, 0), (0, 14, 0), (0, 16, 0), (0, 17, 0), (1, 22, 0), (1, 24, 0), (1, 29, 0), (1, 38, 0), (1, 13, 1),
-        (1, 31, 0), (1, 32, 0), (0, 9, 1), (0, 10, 1), (0, 11, 1), (0, 14, 1), (0, 16, 1), (0, 18, 0), (1, 22, 1),
-        (1, 29, 1), (1, 35, 0), (1, 25, 0), (1, 12, 2), (1, 13, 2), (1, 19, 0), (1, 39, 0), (0, 7, 0), (0, 10, 2),
-        (0, 11, 2), (0, 14, 2), (0, 16, 2), (0, 17, 1), (1, 29, 2), (1, 22, 2), (1, 12, 3), (1, 13, 3), (1, 15, 2),
-        (1, 37, 0), (0, 9, 2), (0, 10, 3), (0, 11, 3), (0, 14, 3), (0, 16, 3), (0, 18, 1), (1, 29, 3), (1, 30, 0),
-        (1, 8, 0), (1, 27, 0), (0, 6, 0), (0, 12, 0), (0, 13, 0), (0, 15, 0), (0, 17, 2), (1, 28, 0), (0, 29, 0),
-        (1, 45, 0), (1, 48, 0), (1, 27, 1), (1, 38, 1), (0, 22, 0), (0, 24, 0), (0, 12, 1), (0, 15, 1), (0, 38, 0),
-        (1, 44, 0), (1, 28, 1), (1, 53, 0), (1, 30, 1), (0, 29, 1), (1, 45, 1), (1, 7, 1), (1, 27, 2), (1, 15, 3),
-        (1, 31, 1), (0, 22, 1), (0, 13, 1), (0, 31, 0), (0, 32, 0), (0, 35, 0), (1, 49, 0), (0, 29, 2), (1, 45, 2),
-        (1, 25, 1), (1, 27, 3), (1, 18, 2), (0, 25, 0), (0, 12, 2), (0, 13, 2), (0, 19, 0), (0, 39, 0), (1, 28, 2),
-        (1, 30, 2), (0, 29, 3), (1, 45, 3), (1, 24, 1), (1, 32, 1), (1, 50, 0), (1, 54, 0), (0, 22, 2), (0, 12, 3),
-        (0, 13, 3), (0, 15, 2), (0, 37, 0), (1, 28, 3), (1, 30, 3), (0, 30, 0), (1, 26, 0), (1, 20, 0), (1, 52, 0),
-        (0, 8, 0), (0, 27, 0), (0, 28, 0), (0, 45, 0), (0, 48, 0),
+        (0, 3, 0), (0, 4, 0), (0, 5, 0), (1, 6, 0), (1, 8, 0), (1, 10, 0), (1, 11, 0), (1, 15, 0), (1, 16, 0),
+        (1, 9, 0), (1, 17, 0), (0, 0, 1), (0, 1, 1), (0, 2, 1), (0, 3, 1), (0, 4, 1), (0, 5, 1), (1, 6, 1),
+        (1, 10, 1), (1, 11, 1), (1, 15, 1), (1, 7, 0), (1, 18, 0), (0, 0, 2), (0, 1, 2), (0, 2, 2), (0, 3, 2),
+        (0, 4, 2), (0, 5, 2), (1, 6, 2), (1, 10, 2), (1, 11, 2), (1, 15, 2), (1, 8, 1), (1, 16, 1), (0, 0, 3),
+        (0, 1, 3), (0, 2, 3), (0, 3, 3), (0, 4, 3), (0, 5, 3), (1, 6, 3), (1, 10, 3), (1, 11, 3), (1, 15, 3),
+        (1, 9, 1), (1, 12, 0), (1, 13, 0), (1, 14, 0), (1, 17, 1), (1, 13, 1), (1, 14, 1), (0, 6, 0), (0, 8, 0),
+        (0, 10, 0), (0, 11, 0), (0, 15, 0), (0, 16, 0), (1, 22, 0), (1, 29, 0), (1, 31, 0), (1, 32, 0), (1, 12, 1),
+        (1, 13, 2), (1, 14, 2), (0, 6, 1), (0, 9, 0), (0, 10, 1), (0, 11, 1), (0, 15, 1), (0, 17, 0), (1, 22, 1),
+        (1, 29, 1), (1, 38, 0), (1, 24, 0), (1, 26, 0), (1, 12, 2), (1, 14, 3), (1, 18, 1), (0, 6, 2), (0, 7, 0),
+        (0, 10, 2), (0, 11, 2), (0, 15, 2), (0, 18, 0), (1, 29, 2), (1, 12, 3), (1, 13, 3), (1, 16, 2), (1, 35, 0),
+        (1, 39, 0), (0, 6, 3), (0, 8, 1), (0, 10, 3), (0, 11, 3), (0, 15, 3), (0, 16, 1), (1, 29, 3), (1, 22, 2),
+        (1, 17, 2), (0, 9, 1), (0, 12, 0), (0, 13, 0), (0, 14, 0), (0, 17, 1), (1, 27, 0), (1, 28, 0), (1, 30, 0),
+        (0, 29, 0), (1, 45, 0), (1, 7, 1), (1, 32, 1), (1, 19, 0), (0, 22, 0), (0, 13, 1), (0, 14, 1), (0, 31, 0),
+        (0, 32, 0), (1, 44, 0), (1, 30, 1), (1, 49, 0), (0, 29, 1), (1, 45, 1), (1, 26, 1), (1, 28, 1), (1, 20, 0),
+        (0, 22, 1), (0, 12, 1), (0, 13, 2), (0, 14, 2), (0, 38, 0), (1, 30, 2), (1, 27, 1), (0, 29, 2), (1, 45, 2),
+        (1, 28, 2), (1, 37, 0), (1, 51, 0), (0, 24, 0), (0, 26, 0), (0, 12, 2), (0, 14, 3), (0, 18, 1), (1, 30, 3),
+        (1, 27, 2), (0, 29, 3), (1, 45, 3), (1, 8, 2), (1, 28, 3), (1, 46, 0), (1, 38, 1), (1, 53, 0), (0, 12, 3),
+        (0, 13, 3), (0, 16, 2), (0, 35, 0), (0, 39, 0), (1, 27, 3), (0, 27, 0), (1, 31, 1), (1, 34, 0), (1, 52, 0),
+        (0, 22, 2), (0, 28, 0), (0, 30, 0), (0, 45, 0), (0, 17, 2),
     ),
     (
         (1, 44, 1), (0, 44, 0), (1, 56, 0), (1, 61, 0),
     ),
     (
-        (1, 9, 3), (1, 46, 0), (1, 34, 0), (1, 47, 0), (1, 40, 0), (0, 27, 1), (0, 28, 1), (0, 45, 1), (0, 38, 1),
-        (0, 53, 0), (1, 36, 0), (0, 30, 1),
-    ),
-    (
-        (1, 22, 3), (1, 23, 0), (1, 17, 3), (1, 35, 1), (0, 7, 1), (0, 27, 2), (0, 15, 3), (0, 45, 2), (0, 31, 1),
-        (1, 21, 0), (0, 49, 0), (1, 57, 0),
-    ),
-    (
-        (1, 6, 1), (1, 42, 0), (1, 33, 0), (1, 19, 1), (1, 39, 1), (0, 25, 1), (0, 27, 3), (0, 28, 2), (0, 45, 3),
-        (0, 18, 2), (0, 30, 2),
-    ),
-    (
-        (1, 41, 0), (1, 26, 1), (1, 37, 1), (1, 59, 0), (0, 24, 1), (0, 28, 3), (0, 32, 1), (0, 50, 0), (0, 54, 0),
-        (1, 49, 1), (1, 53, 1), (1, 51, 0), (0, 30, 3),
-    ),
-    (
-        (1, 48, 1), (1, 60, 0), (0, 26, 0), (0, 56, 0), (0, 20, 0), (0, 52, 0), (0, 61, 0), (1, 43, 0), (1, 62, 0),
-        (1, 58, 0), (0, 44, 1), (1, 56, 1),
-    ),
-    (
-        (1, 8, 1), (1, 24, 2), (1, 32, 2), (1, 34, 1), (1, 38, 2), (0, 9, 3), (0, 46, 0), (0, 34, 0), (0, 47, 0),
-        (0, 40, 0), (1, 55, 0), (0, 36, 0),
-    ),
-    (
-        (1, 7, 2), (1, 31, 2), (1, 35, 2), (1, 52, 1), (0, 22, 3), (0, 23, 0), (0, 17, 3), (0, 35, 1), (0, 57, 0),
-        (1, 47, 1), (1, 44, 2), (0, 21, 0), (1, 25, 2), (1, 46, 1), (1, 18, 3), (1, 19, 2), (0, 6, 1), (0, 42, 0),
-        (0, 33, 0), (0, 19, 1), (0, 39, 1),
-    ),
-    (
-        (1, 36, 1), (0, 49, 1), (1, 57, 1), (1, 23, 1), (1, 26, 2), (1, 33, 1), (1, 50, 1), (1, 54, 1), (0, 41, 0),
-        (0, 26, 1), (0, 37, 1), (0, 53, 1), (0, 59, 0),
-    ),
-    (
-        (1, 21, 1), (0, 51, 0), (1, 41, 1), (1, 42, 1), (1, 20, 1), (1, 60, 1), (0, 43, 0), (0, 56, 1), (0, 48, 1),
-        (0, 60, 0), (0, 62, 0), (1, 62, 1),
-    ),
-    (
-        (0, 58, 0), (1, 43, 1), (1, 32, 3), (1, 34, 2), (1, 40, 1), (1, 61, 1), (0, 8, 1), (0, 24, 2), (0, 32, 2),
-        (0, 34, 1), (0, 38, 2), (1, 49, 2),
-    ),
-    (
-        (1, 51, 1), (0, 55, 0), (1, 19, 3), (1, 39, 2), (1, 53, 2), (1, 59, 1), (0, 7, 2), (0, 31, 2), (0, 35, 2),
-        (0, 47, 1), (0, 52, 1), (1, 58, 1),
-    ),
-    (
-        (0, 44, 2), (1, 56, 2), (1, 6, 2), (1, 24, 3), (1, 47, 2), (1, 37, 2), (0, 25, 2), (0, 46, 1), (0, 18, 3),
-        (0, 19, 2), (0, 57, 1), (1, 35, 3), (1, 55, 1),
-    ),
-    (
-        (0, 36, 1), (1, 8, 2), (1, 26, 3), (1, 33, 2), (1, 48, 2), (1, 52, 2), (0, 23, 1), (0, 26, 2), (0, 33, 1),
-        (0, 50, 1), (0, 54, 1), (1, 44, 3),
-    ),
-    (
-        (0, 21, 1), (1, 7, 3), (1, 46, 2), (1, 34, 3), (1, 38, 3), (0, 41, 1), (0, 42, 1), (0, 20, 1), (0, 60, 1),
-        (0, 62, 1), (1, 36, 2), (0, 49, 2), (1, 57, 2),
-    ),
-    (
-        (1, 41, 2), (1, 23, 2), (1, 25, 3), (1, 31, 3), (0, 43, 1), (0, 32, 3), (0, 34, 2), (0, 40, 1), (0, 61, 1),
-        (1, 49, 3), (0, 51, 1),
-    ),
-    (
-        (1, 42, 2), (1, 33, 3), (1, 50, 2), (0, 56, 2), (0, 19, 3), (0, 39, 2), (0, 53, 2), (0, 59, 1), (1, 60, 2),
-        (1, 62, 2), (1, 21, 2), (0, 58, 1),
-    ),
-    (
-        (1, 43, 2), (1, 20, 2), (1, 54, 2), (0, 6, 2), (0, 24, 3), (0, 35, 3), (0, 47, 2), (0, 37, 2), (1, 47, 3),
-        (1, 51, 2), (0, 55, 1), (1, 40, 2), (1, 59, 2), (1, 61, 2),
-    ),
-    (
-        (0, 8, 2), (0, 26, 3), (0, 33, 2), (0, 48, 2), (0, 52, 2), (1, 58, 2), (0, 44, 3), (1, 56, 3), (1, 41, 3),
-        (1, 39, 3), (1, 53, 3),
-    ),
-    (
-        (0, 7, 3), (0, 46, 2), (0, 34, 3), (0, 57, 2), (0, 38, 3), (1, 52, 3), (1, 55, 2), (0, 36, 2), (1, 6, 3),
-        (1, 37, 3),
-    ),
-    (
-        (0, 41, 2), (0, 23, 2), (0, 25, 3), (0, 31, 3), (1, 46, 3), (1, 36, 3), (0, 49, 3), (0, 60, 2), (1, 57, 3),
-        (1, 8, 3), (1, 23, 3), (1, 48, 3), (0, 42, 2), (0, 33, 3), (0, 50, 2), (0, 62, 2),
-    ),
-    (
-        (1, 21, 3), (0, 21, 2), (1, 42, 3), (1, 50, 3), (1, 54, 3), (0, 43, 2), (0, 47, 3), (0, 20, 2), (0, 54, 2),
-    ),
-    (
-        (0, 51, 2), (1, 43, 3), (1, 20, 3), (0, 56, 3), (0, 40, 2), (0, 59, 2), (0, 61, 2), (1, 62, 3),
-    ),
-    (
-        (0, 58, 2), (1, 40, 3), (1, 61, 3), (0, 41, 3), (0, 39, 3), (0, 52, 3), (0, 53, 3), (1, 51, 3), (1, 59, 3),
-        (1, 60, 3), (1, 58, 3), (0, 55, 2),
-    ),
-    (
-        (0, 6, 3), (0, 46, 3), (0, 57, 3), (0, 37, 3), (1, 55, 3), (0, 36, 3),
-    ),
-    (
-        (0, 8, 3), (0, 23, 3), (0, 48, 3), (0, 21, 3),
-    ),
-    (
-        (0, 42, 3), (0, 50, 3), (0, 54, 3),
-    ),
-    (
-        (0, 43, 3), (0, 20, 3), (0, 62, 3), (0, 51, 3), (0, 60, 3),
-    ),
-    (
-        (0, 40, 3), (0, 59, 3), (0, 61, 3), (0, 58, 3),
-    ),
-    (
-        (0, 55, 3),
-    ),
+        (1, 23, 0), (1, 9, 2), (1, 18, 2), (1, 35, 1), (1, 47, 0), (0, 7, 1), (0, 30, 1), (0, 45, 1), (0, 32, 1),
+        (0, 19, 0), (1, 48, 0), (0, 49, 0),
+    ),
+    (
+        (1, 25, 0), (1, 43, 0), (1, 16, 3), (1, 57, 0), (1, 39, 1), (0, 26, 1), (0, 28, 1), (0, 30, 2), (0, 45, 2),
+        (0, 20, 0), (1, 36, 0), (0, 27, 1),
+    ),
+    (
+        (1, 22, 3), (1, 42, 0), (1, 17, 3), (1, 33, 0), (1, 54, 0), (0, 28, 2), (0, 30, 3), (0, 45, 3), (0, 37, 0),
+        (0, 51, 0), (1, 49, 1), (0, 27, 2),
+    ),
+    (
+        (1, 41, 0), (1, 7, 2), (1, 24, 1), (1, 50, 0), (0, 8, 2), (0, 28, 3), (0, 46, 0), (0, 38, 1), (0, 53, 0),
+        (1, 60, 0), (1, 21, 0), (0, 27, 3),
+    ),
+    (
+        (1, 32, 2), (1, 19, 1), (1, 40, 0), (1, 59, 0), (0, 56, 0), (0, 31, 1), (0, 34, 0), (0, 52, 0), (0, 61, 0),
+        (1, 62, 0), (1, 58, 0), (0, 44, 1),
+    ),
+    (
+        (1, 26, 2), (1, 56, 1), (1, 46, 1), (1, 20, 1), (1, 53, 1), (0, 23, 0), (0, 9, 2), (0, 18, 2), (0, 35, 1),
+        (0, 47, 0), (1, 55, 0), (0, 48, 0),
+    ),
+    (
+        (1, 34, 1), (1, 47, 1), (1, 37, 1), (1, 51, 1), (1, 52, 1), (0, 25, 0), (0, 43, 0), (0, 16, 3), (0, 57, 0),
+        (0, 39, 1), (1, 44, 2), (0, 36, 0), (1, 23, 1), (1, 35, 2), (1, 38, 2), (1, 61, 1), (0, 22, 3), (0, 42, 0),
+        (0, 17, 3), (0, 33, 0), (0, 54, 0),
+    ),
+    (
+        (1, 48, 1), (0, 49, 1), (1, 57, 1), (1, 8, 3), (1, 25, 1), (1, 43, 1), (1, 31, 2), (1, 33, 1), (0, 41, 0),
+        (0, 7, 2), (0, 24, 1), (0, 50, 0), (0, 60, 0),
+    ),
+    (
+        (1, 36, 1), (0, 21, 0), (1, 41, 1), (1, 9, 3), (1, 42, 1), (1, 18, 3), (1, 54, 1), (0, 32, 2), (0, 19, 1),
+        (0, 40, 0), (0, 59, 0), (0, 62, 0), (1, 49, 2),
+    ),
+    (
+        (0, 58, 0), (1, 24, 2), (1, 32, 3), (1, 50, 1), (0, 26, 2), (0, 56, 1), (0, 46, 1), (0, 20, 1), (0, 53, 1),
+        (1, 60, 1), (1, 62, 1), (1, 21, 1), (0, 55, 0),
+    ),
+    (
+        (1, 19, 2), (1, 39, 2), (1, 40, 1), (1, 59, 1), (0, 34, 1), (0, 47, 1), (0, 37, 1), (0, 51, 1), (0, 52, 1),
+        (1, 58, 1), (0, 44, 2), (1, 56, 2),
+    ),
+    (
+        (1, 7, 3), (1, 20, 2), (0, 23, 1), (0, 35, 2), (0, 57, 1), (0, 38, 2), (0, 61, 1), (1, 47, 2), (1, 52, 2),
+        (1, 53, 2), (1, 55, 1), (0, 48, 1),
+    ),
+    (
+        (1, 26, 3), (1, 33, 2), (1, 34, 2), (1, 37, 2), (0, 8, 3), (0, 25, 1), (0, 43, 1), (0, 31, 2), (0, 33, 1),
+        (1, 46, 2), (1, 44, 3), (0, 36, 1),
+    ),
+    (
+        (1, 23, 2), (1, 51, 2), (1, 38, 3), (0, 41, 1), (0, 9, 3), (0, 42, 1), (0, 18, 3), (0, 54, 1), (1, 35, 3),
+        (1, 48, 2), (0, 49, 2), (1, 57, 2),
+    ),
+    (
+        (1, 41, 2), (1, 25, 2), (1, 43, 2), (1, 31, 3), (1, 61, 2), (0, 24, 2), (0, 32, 3), (0, 50, 1), (0, 60, 1),
+        (0, 62, 1), (1, 36, 2), (0, 21, 1),
+    ),
+    (
+        (1, 42, 2), (1, 33, 3), (1, 50, 2), (0, 56, 2), (0, 19, 2), (0, 39, 2), (0, 40, 1), (0, 59, 1), (1, 54, 2),
+        (1, 62, 2), (1, 49, 3), (0, 58, 1),
+    ),
+    (
+        (1, 41, 3), (1, 24, 3), (1, 19, 3), (1, 39, 3), (0, 7, 3), (0, 47, 2), (0, 20, 2), (0, 52, 2), (0, 53, 2),
+        (1, 60, 2), (1, 21, 2), (0, 55, 1), (1, 51, 3), (1, 20, 3), (1, 40, 2), (1, 59, 2),
+    ),
+    (
+        (0, 26, 3), (0, 46, 2), (0, 33, 2), (0, 34, 2), (0, 37, 2), (1, 58, 2), (0, 44, 3), (1, 56, 3), (1, 37, 3),
+        (1, 61, 3), (0, 23, 2), (0, 35, 3), (0, 57, 2), (0, 51, 2), (0, 38, 3),
+    ),
+    (
+        (1, 47, 3), (1, 52, 3), (1, 53, 3), (1, 55, 2), (0, 48, 2), (1, 34, 3), (0, 41, 2), (0, 25, 2), (0, 43, 2),
+        (0, 31, 3), (0, 61, 2), (1, 46, 3), (1, 50, 3), (1, 48, 3), (0, 36, 2),
+    ),
+    (
+        (1, 23, 3), (1, 25, 3), (0, 42, 2), (0, 33, 3), (0, 50, 2), (0, 54, 2), (0, 62, 2), (1, 36, 3), (0, 49, 3),
+        (1, 57, 3),
+    ),
+    (
+        (1, 43, 3), (0, 41, 3), (0, 24, 3), (0, 19, 3), (0, 39, 3), (0, 60, 2), (1, 54, 3), (1, 21, 3), (0, 21, 2),
+    ),
+    (
+        (1, 42, 3), (0, 56, 3), (0, 51, 3), (0, 20, 3), (0, 40, 2), (0, 59, 2), (1, 40, 3), (1, 62, 3), (0, 58, 2),
+    ),
+    (
+        (0, 47, 3), (0, 37, 3), (0, 52, 3), (0, 53, 3), (0, 61, 3), (1, 58, 3), (1, 59, 3), (1, 60, 3), (1, 55, 3),
+        (0, 55, 2),
+    ),
+    (
+        (0, 46, 3), (0, 34, 3), (0, 50, 3), (0, 48, 3), (0, 57, 3),
+    ),
+    (
+        (0, 23, 3), (0, 25, 3), (0, 36, 3),
+    ),
+    (
+        (0, 43, 3), (0, 54, 3), (0, 21, 3), (0, 62, 3),
+    ),
+    (
+        (0, 42, 3), (0, 40, 3), (0, 58, 3),
+    ),
+    (
+        (0, 59, 3), (0, 60, 3), (0, 55, 3),
+    ),
+    (),
     (),
     (),
     (),
@@ -473,7 +471,8 @@
     def peaked():
         scales[1:2, :] = jnp.max(tops[...], axis=0, keepdims=True) * scales[0:1, :]
 
-    def folded(g, half):
+    def folded(g, piece):
+        half = piece // 2
         scale = jnp.broadcast_to(scales[0:1, :], (8, 256))
         peaks = jnp.broadcast_to(scales[1:2, :], (8, 256))
         sublane = lax.broadcasted_iota(jnp.int32, (8, 256), 0)
@@ -483,18 +482,18 @@
         local = jnp.where(local < nwords, local, -8)
         local = spread(jnp.where(segment == core * GROUPS + g, local, 0))
         wanted = jnp.broadcast_to(jnp.concatenate([local, local], axis=1), (8, 256)) - sublane
-        if half == 0:
+        if piece == 0:
             mass = moment = picked = jnp.zeros((8, 256), F32)
         else:
             mass, moment, picked = (sums[k] for k in range(3))
-        for k in range(150):
+        for k in range(75 * (piece % 2), 75 * (piece % 2) + 75):
             z_all = final[half, 8 * k : 8 * k + 8, :] * scale
             z_rel = z_all - peaks
             e = jnp.exp(z_rel)
             mass = mass + e
             moment = moment + e * z_rel
             picked = jnp.where(wanted == 8 * k, z_all, picked)
-        if half == 0:
+        if piece < 3:
             for k, value in enumerate((mass, moment, picked)):
                 sums[k] = value
             return
@@ -548,16 +547,16 @@
                     pl.when(g == 0)(functools.partial(words_ready, p))
                 multiply(g, p, k, now)
                 prepare(*following, k, later)
-                if p == 1:
-                    folded(former_group, k)
+                if p < 3:
+                    folded(former_group, 2 * (p - 1) + k)
             if p == 3:
                 peaked()
         return carry
 
     lax.fori_loop(0, GROUPS, body, 0)
     run(PLAN[34])
-    for half in range(2):
-        folded(GROUPS - 1, half)
+    for piece in range(4):
+        folded(GROUPS - 1, piece)
 
     def joined(parts):
         most = functools.reduce(jnp.maximum, [part[0] for part in parts])

time: 76.9 us -> 75.3 us (0.979)
  Pallas kernels: 74.9 us -> 73.3 us
    pallas_call x1, Pallas kernels: 74.9 us -> 73.3 us  [shards(): pl.pallas_call(kernel, out_shape=jax.ShapeDtypeStruct((3, 2, 128), F32),...]
where the time goes in v4:
time: 75.3 us; the launch traced here: 75.2 us
  Pallas kernels  73.3 us (97%)
  local copies, waits for them, and re-layouts  1.25 us (2%)
    pallas_call x1, Pallas kernels, shards(): pl.pallas_call(kernel, out_shape=jax.ShapeDtypeStruct((3, 2, 128), F32),...  73.3 us

profile of v4, /device:TPU:1, one launch (start us, length us, event | category | flops | bytes accessed | tf_op | source)
XLA Modules:
  0.0 75.2 jit_solution(3412610471396828401)
XLA Ops:
  0.6 73.3 %shard_map.76 = f32[3,2,128]{2,1,0:T(2,128)} custom-call(bf16[320,128]{1,0:T(8,128)(2,1)} %bitcast.9, bf16[2,320,128]{2,1,0:T(8,128)(2,1)} %bitcast.8, f32[320]{0:T(512)} %gain_hbm.1, bf16[1188,5120]{1,0:T(8,128)(2,1)} %unembed_hbm.1, s32[128]{0:T(128)} %targets_hbm.1), custom_call_target="tpu_custom_call" | custom-call | tf_op jit(solution)/shard_map/pallas_call | solution.py:685
  73.9 1.2 %slice_bitcast_fusion = (f32[2,128]{1,0:T(2,128)}, f32[2,128]{1,0:T(2,128)}, f32[2,128]{1,0:T(2,128)}) fusion(f32[3,2,128]{2,1,0:T(2,128)} %shard_map.76), kind=kLoop, calls=%fused_computation | loop fusion | bytes 6144 | tf_op jit(solution)/shard_map/squeeze | solution.py:732

commit v5 on v4

--- a/solution.py
+++ b/solution.py
@@ -398,7 +398,7 @@
             )
         )
 
-    for copy in their_words:
+    for copy in their_words[:2]:
         copy.start()
 
     segment = lax.broadcasted_iota(jnp.int32, (1, 128), 1) // GTOK
@@ -515,6 +515,8 @@
         ).wait_recv()
 
     run(PLAN[0])
+    for copy in their_words[2:]:
+        copy.start()
     part.wait_recv()
     for zp in range(2):
         prepare(0, 0, zp, rows_c)

time: 75.3 us -> 75.3 us (level)
  no operation moved by 1% of the time
where the time goes in v5:
time: 75.3 us; the launch traced here: 75.2 us
  Pallas kernels  73.3 us (97%)
  local copies, waits for them, and re-layouts  1.25 us (2%)
    pallas_call x1, Pallas kernels, shards(): pl.pallas_call(kernel, out_shape=jax.ShapeDtypeStruct((3, 2, 128), F32),...  73.3 us

profile of v5, /device:TPU:1, one launch (start us, length us, event | category | flops | bytes accessed | tf_op | source)
XLA Modules:
  0.0 75.2 jit_solution(6605289959169003242)
XLA Ops:
  0.6 73.3 %shard_map.76 = f32[3,2,128]{2,1,0:T(2,128)} custom-call(bf16[320,128]{1,0:T(8,128)(2,1)} %bitcast.9, bf16[2,320,128]{2,1,0:T(8,128)(2,1)} %bitcast.8, f32[320]{0:T(512)} %gain_hbm.1, bf16[1188,5120]{1,0:T(8,128)(2,1)} %unembed_hbm.1, s32[128]{0:T(128)} %targets_hbm.1), custom_call_target="tpu_custom_call" | custom-call | tf_op jit(solution)/shard_map/pallas_call | solution.py:687
  73.9 1.2 %slice_bitcast_fusion = (f32[2,128]{1,0:T(2,128)}, f32[2,128]{1,0:T(2,128)}, f32[2,128]{1,0:T(2,128)}) fusion(f32[3,2,128]{2,1,0:T(2,128)} %shard_map.76), kind=kLoop, calls=%fused_computation | loop fusion | bytes 6144 | tf_op jit(solution)/shard_map/squeeze | solution.py:734
